TPU v7x, 16 devices: a 4x2x1 block of a 4x4x8 slice. The times are simulated.
16 devices in a mesh: dp: 2 (over y, z), cp: 8 (over x, core).
Axes of the slice: x: 4, y: 2, z: 1, core: 2. Of those that a mesh axis runs over, the one named last changes fastest.
The devices are a block of a 4x4x8 slice.
Arguments:
- query: bfloat16 [8, 256, 32, 128], P('dp', 'cp'), parts along dimension 0
- key: bfloat16 [8, 256, 128], P('dp', 'cp'), parts along dimension 0
- value: bfloat16 [8, 256, 128], P('dp', 'cp'), parts along dimension 0
- positions: int32 [512], P(('dp', 'cp')), parts along dimension 0
- grad_out: bfloat16 [8, 256, 32, 128], P('dp', 'cp'), parts along dimension 0
Outputs:
- output 1: bfloat16 [8, 256, 32, 128], P('dp', 'cp'), parts along dimension 0
- output 2: bfloat16 [8, 256, 32, 128], P('dp', 'cp'), parts along dimension 0
- output 3: bfloat16 [8, 256, 128], P('dp', 'cp'), parts along dimension 0
- output 4: bfloat16 [8, 256, 128], P('dp', 'cp'), parts along dimension 0
There are 2 independent parts. A program takes and returns all parts, laid end to end along the dimension named above; each array names one.
All inputs are finite; a program needn't handle non-finite values.
Results may differ from a plain program's by a relative error of at most 0.00834231.
Values are sent between devices in bfloat16 or wider.
A program may use at most 768 MiB of HBM per device.

v0:
```python
import jax
import jax.numpy as jnp
from jax import lax
from jax.sharding import PartitionSpec as P

ROPE_BASE = 10000


def rope_tables(positions, head):
    half_dim = head // 2
    inv_freq = jnp.power(jnp.float32(ROPE_BASE), -2.0 * jnp.arange(half_dim, dtype=jnp.float32) / head)
    angles = positions.astype(jnp.float32)[..., None] * inv_freq
    angles = jnp.concatenate([angles, angles], axis=-1)
    return jnp.cos(angles), jnp.sin(angles)


def rotate(values, cos_tab, sin_tab):
    half_dim = values.shape[-1] // 2
    turned = jnp.concatenate([-values[..., half_dim:], values[..., :half_dim]], axis=-1)
    return values * cos_tab + turned * sin_tab


def solution(mesh):
    cp_size = mesh.shape['cp']
    shift_pairs = [(source, (source + 1) % cp_size) for source in range(cp_size)]
    query_spec = P('dp', 'cp', None, None)
    kv_spec = P('dp', 'cp', None)
    pos_spec = P(('dp', 'cp'))

    def per_device(query, key, value, positions, grad_out):
        batch, blk_len, heads, head = query.shape
        scale = head ** -0.5
        my_idx = lax.axis_index('cp')
        cos_tab, sin_tab = rope_tables(positions, head)
        cos_q = cos_tab[None, :, None, :]
        sin_q = sin_tab[None, :, None, :]
        query_rot = rotate(query, cos_q, sin_q).astype(jnp.bfloat16)
        key_rot = rotate(key, cos_tab[None], sin_tab[None]).astype(jnp.bfloat16)
        local_idx = jnp.arange(blk_len)
        diag_mask = (local_idx[None, :] <= local_idx[:, None])[None, :, None, :]

        def block_scores(key_blk, causal_mask):
            scores = jnp.einsum('crie,cle->cril', query_rot, key_blk, preferred_element_type=jnp.float32) * scale
            if causal_mask is None:
                return scores
            return jnp.where(causal_mask, scores, -jnp.inf)

        def forward_block(key_blk, value_blk, state, causal_mask):
            run_max, run_sum, out_acc = state
            scores = block_scores(key_blk, causal_mask)
            new_max = jnp.maximum(run_max, jnp.max(scores, axis=-1))
            factor = jnp.exp(run_max - new_max)
            weights = jnp.exp(scores - new_max[..., None])
            run_sum = run_sum * factor + jnp.sum(weights, axis=-1)
            out_acc = out_acc * factor[..., None] + jnp.einsum('cril,cle->crie', weights.astype(jnp.bfloat16), value_blk, preferred_element_type=jnp.float32)
            return new_max, run_sum, out_acc

        init_state = (jnp.full((batch, blk_len, heads), -jnp.inf, jnp.float32), jnp.zeros((batch, blk_len, heads), jnp.float32), jnp.zeros((batch, blk_len, heads, head), jnp.float32))
        state = forward_block(key_rot, value, init_state, diag_mask)

        def forward_step(step, carry):
            key_blk, value_blk, state_in = carry
            key_blk, value_blk = lax.ppermute((key_blk, value_blk), 'cp', shift_pairs)
            state_out = lax.cond(step <= my_idx, lambda prev: forward_block(key_blk, value_blk, prev, None), lambda prev: prev, state_in)
            return key_blk, value_blk, state_out

        fwd_carry = lax.fori_loop(1, cp_size, forward_step, (key_rot, value, state))
        run_max, run_sum, out_acc = fwd_carry[2]
        attn_out = (out_acc / run_sum[..., None]).astype(jnp.bfloat16)
        log_sum = run_max + jnp.log(run_sum)
        delta = jnp.einsum('bqhd,bqhd->bqh', grad_out, attn_out, preferred_element_type=jnp.float32)

        def backward_block(key_blk, value_blk, grads, causal_mask):
            dquery_acc, dkey_blk, dvalue_blk = grads
            scores = block_scores(key_blk, causal_mask)
            probs_f = jnp.exp(scores - log_sum[..., None])
            dprobs = jnp.einsum('crie,cle->cril', grad_out, value_blk, preferred_element_type=jnp.float32)
            dscore = (probs_f * (dprobs - delta[..., None])).astype(jnp.bfloat16)
            dquery_acc = dquery_acc + jnp.einsum('cril,cle->crie', dscore, key_blk, preferred_element_type=jnp.float32) * scale
            dkey_blk = dkey_blk + jnp.einsum('cril,crie->cle', dscore, query_rot, preferred_element_type=jnp.float32) * scale
            dvalue_blk = dvalue_blk + jnp.einsum('cril,crie->cle', probs_f.astype(jnp.bfloat16), grad_out, preferred_element_type=jnp.float32)
            return dquery_acc, dkey_blk, dvalue_blk

        zero_kv = jnp.zeros((batch, blk_len, head), jnp.float32)
        grads = backward_block(key_rot, value, (jnp.zeros((batch, blk_len, heads, head), jnp.float32), zero_kv, zero_kv), diag_mask)

        def backward_step(step, carry):
            key_blk, value_blk, dquery_acc, dkey_blk, dvalue_blk = carry
            key_blk, value_blk, dkey_blk, dvalue_blk = lax.ppermute((key_blk, value_blk, dkey_blk, dvalue_blk), 'cp', shift_pairs)
            grads_new = lax.cond(step <= my_idx, lambda prev: backward_block(key_blk, value_blk, prev, None), lambda prev: prev, (dquery_acc, dkey_blk, dvalue_blk))
            return (key_blk, value_blk) + tuple(grads_new)

        bwd_carry = lax.fori_loop(1, cp_size, backward_step, (key_rot, value) + tuple(grads))
        dkey_home, dvalue_home = lax.ppermute((bwd_carry[3], bwd_carry[4]), 'cp', shift_pairs)
        grad_query = rotate(bwd_carry[2], cos_q, -sin_q).astype(jnp.bfloat16)
        grad_key = rotate(dkey_home, cos_tab[None], -sin_tab[None]).astype(jnp.bfloat16)
        return attn_out, grad_query, grad_key, dvalue_home.astype(jnp.bfloat16)

    return jax.shard_map(per_device, mesh=mesh, in_specs=(query_spec, kv_spec, kv_spec, pos_spec, query_spec), out_specs=(query_spec, query_spec, kv_spec, kv_spec), check_vma=False)
```

profile of v0, /device:TPU:113, one launch (start us, length us, event | category | flops | bytes accessed | tf_op | source)
XLA Modules:
  0.0 155.9 jit_solution(11249896040888537385)
XLA Ops:
  2.9 2.1 %slice_negate_fusion.1 = (bf16[4,32,32,64]{3,2,1,0:T(8,128)(2,1)S(1)}, bf16[4,32,32,64]{3,2,1,0:T(8,128)(2,1)S(1)}) fusion(bf16[4,32,32,128]{3,2,1,0:T(8,128)(2,1)} %param.13), kind=kLoop, calls=%fused_computation.55 | loop fusion | flops 262144 | bytes 2097152 | tf_op jit(solution)/shard_map/neg | solution.py:19
  6.1 1.9 %fusion.46 = (f32[4,32,32]{2,1,0:T(8,128)S(1)}, f32[4,32,32,32]{2,3,1,0:T(8,128)S(1)}) fusion(bf16[4,32,32,128]{3,2,1,0:T(8,128)(2,1)S(1)} %add_convert_fusion, bf16[4,32,128]{2,1,0:T(8,128)(2,1)S(1)} %add_convert_fusion.1, pred[32,32]{1,0:T(8,128)(4,1)S(1)} %iota_compare_fusion), kind=kOutput, calls=%fused_computation.76 | convolution fusion | flops 33943552 | bytes 1623040 | tf_op jit(solution)/shard_map/crie,cle->cril/dot_general | solution.py:43
  9.3 1.0 convolution_add_fusion
  10.4 43.4 %while.42 = (s32[]{:T(128)}, bf16[4,32,128]{2,1,0:T(8,128)(2,1)S(1)}, bf16[4,32,128]{2,1,0:T(8,128)(2,1)S(1)}, f32[4,32,32]{2,1,0:T(8,128)S(1)}, f32[4,32,32]{2,...) while((s32[]{:T(128)}, ...), condition=%wide.region_7.8_spmd, body=%wide.region_2.7_spmd.sunk | while | flops 69214208 | bytes 7536931 | solution.py:67
  10.4 2.7 %collective-permute-start = (bf16[4,32,128]{2,1,0:T(8,128)(2,1)S(1)}, bf16[4,32,128]{2,1,0:T(8,128)(2,1)S(1)}, u32[]{:S(2)}, u32[]{:S(2)}) collective-permute-start(bf16[4,32,128]{2,1,0:T(8,128)(2,1)S(1)} %get-tuple-element.632), channel_id=1, source_target_pairs={{0,1},{1,2},{2,3},{3,4},{4,5},{5,6},{6,7},{7,0},{8,9},{9,10},{10,1... | collective-permute-start | bytes 98312 | tf_op jit(solution)/shard_map/while/body/eval_jaxpr/ppermute | solution.py:63
  14.5 3.8 %conditional.4 = ((f32[4,32,32]{2,1,0:T(8,128)S(1)}, f32[4,32,32]{2,1,0:T(8,128)S(1)}, f32[4,32,32,128]{3,2,1,0:T(8,128)S(1)})) conditional(s32[]{:T(128)} %convert_element_type.101, (f32[4,32,32]{2,1,0:T(8,128)S(1)}, f32[4,32,32]{2,1,0:T(8,128)S(1)}, f32[4,32,32,128]{3,2,1,0:T(8,128)S(1)}) %tuple.84, (bf16[4,32,32,128]{3,2,1,0:T(8,128)(2,1)S(1)}, ...), branch_computations={%region_3.3_spmd, %region_4.6_spmd} | conditional | flops 69214208 | bytes 7143456 | solution.py:64
  14.5 1.8 %multiply_reduce_fusion = (f32[4,32,32]{2,1,0:T(8,128)S(1)}, f32[4,32,32,32]{2,3,1,0:T(8,128)S(1)}) fusion(bf16[4,32,32,128]{3,2,1,0:T(8,128)(2,1)S(1)} %get-tuple-element.355, bf16[4,32,128]{2,1,0:T(8,128)(2,1)S(1)} %get-tuple-element.356), kind=kOutput, calls=%fused_computation.2 | convolution fusion | flops 33812480 | bytes 1622016 | tf_op jit(solution)/shard_map/while/body/eval_jaxpr/cond/branch_1_fun/crie,cle->cril/dot_general | solution.py:43
  17.0 1.2 multiply_add_fusion
  18.3 2.4 %collective-permute-start = (bf16[4,32,128]{2,1,0:T(8,128)(2,1)S(1)}, bf16[4,32,128]{2,1,0:T(8,128)(2,1)S(1)}, u32[]{:S(2)}, u32[]{:S(2)}) collective-permute-start(bf16[4,32,128]{2,1,0:T(8,128)(2,1)S(1)} %get-tuple-element.632), channel_id=1, source_target_pairs={{0,1},{1,2},{2,3},{3,4},{4,5},{5,6},{6,7},{7,0},{8,9},{9,10},{10,1... | collective-permute-start | bytes 98312 | tf_op jit(solution)/shard_map/while/body/eval_jaxpr/ppermute | solution.py:63
  22.0 6.2 %collective-permute-start = (bf16[4,32,128]{2,1,0:T(8,128)(2,1)S(1)}, bf16[4,32,128]{2,1,0:T(8,128)(2,1)S(1)}, u32[]{:S(2)}, u32[]{:S(2)}) collective-permute-start(bf16[4,32,128]{2,1,0:T(8,128)(2,1)S(1)} %get-tuple-element.632), channel_id=1, source_target_pairs={{0,1},{1,2},{2,3},{3,4},{4,5},{5,6},{6,7},{7,0},{8,9},{9,10},{10,1... | collective-permute-start | bytes 98312 | tf_op jit(solution)/shard_map/while/body/eval_jaxpr/ppermute | solution.py:63
  29.6 2.4 %collective-permute-start = (bf16[4,32,128]{2,1,0:T(8,128)(2,1)S(1)}, bf16[4,32,128]{2,1,0:T(8,128)(2,1)S(1)}, u32[]{:S(2)}, u32[]{:S(2)}) collective-permute-start(bf16[4,32,128]{2,1,0:T(8,128)(2,1)S(1)} %get-tuple-element.632), channel_id=1, source_target_pairs={{0,1},{1,2},{2,3},{3,4},{4,5},{5,6},{6,7},{7,0},{8,9},{9,10},{10,1... | collective-permute-start | bytes 98312 | tf_op jit(solution)/shard_map/while/body/eval_jaxpr/ppermute | solution.py:63
  32.0 3.2 %collective-permute-start.1 = (bf16[4,32,128]{2,1,0:T(8,128)(2,1)S(1)}, bf16[4,32,128]{2,1,0:T(8,128)(2,1)S(1)}, u32[]{:S(2)}, u32[]{:S(2)}) collective-permute-start(bf16[4,32,128]{2,1,0:T(8,128)(2,1)S(1)} %get-tuple-element.633), channel_id=1, source_target_pairs={{0,1},{1,2},{2,3},{3,4},{4,5},{5,6},{6,7},{7,0},{8,9},{9,10},{10,1... | collective-permute-start | bytes 98312 | tf_op jit(solution)/shard_map/while/body/eval_jaxpr/ppermute | solution.py:63
  35.2 1.0 collective-permute-done.1
  36.2 2.4 %collective-permute-start = (bf16[4,32,128]{2,1,0:T(8,128)(2,1)S(1)}, bf16[4,32,128]{2,1,0:T(8,128)(2,1)S(1)}, u32[]{:S(2)}, u32[]{:S(2)}) collective-permute-start(bf16[4,32,128]{2,1,0:T(8,128)(2,1)S(1)} %get-tuple-element.632), channel_id=1, source_target_pairs={{0,1},{1,2},{2,3},{3,4},{4,5},{5,6},{6,7},{7,0},{8,9},{9,10},{10,1... | collective-permute-start | bytes 98312 | tf_op jit(solution)/shard_map/while/body/eval_jaxpr/ppermute | solution.py:63
  40.0 6.0 %collective-permute-start = (bf16[4,32,128]{2,1,0:T(8,128)(2,1)S(1)}, bf16[4,32,128]{2,1,0:T(8,128)(2,1)S(1)}, u32[]{:S(2)}, u32[]{:S(2)}) collective-permute-start(bf16[4,32,128]{2,1,0:T(8,128)(2,1)S(1)} %get-tuple-element.632), channel_id=1, source_target_pairs={{0,1},{1,2},{2,3},{3,4},{4,5},{5,6},{6,7},{7,0},{8,9},{9,10},{10,1... | collective-permute-start | bytes 98312 | tf_op jit(solution)/shard_map/while/body/eval_jaxpr/ppermute | solution.py:63
  47.5 2.4 %collective-permute-start = (bf16[4,32,128]{2,1,0:T(8,128)(2,1)S(1)}, bf16[4,32,128]{2,1,0:T(8,128)(2,1)S(1)}, u32[]{:S(2)}, u32[]{:S(2)}) collective-permute-start(bf16[4,32,128]{2,1,0:T(8,128)(2,1)S(1)} %get-tuple-element.632), channel_id=1, source_target_pairs={{0,1},{1,2},{2,3},{3,4},{4,5},{5,6},{6,7},{7,0},{8,9},{9,10},{10,1... | collective-permute-start | bytes 98312 | tf_op jit(solution)/shard_map/while/body/eval_jaxpr/ppermute | solution.py:63
  49.9 2.9 %collective-permute-start.1 = (bf16[4,32,128]{2,1,0:T(8,128)(2,1)S(1)}, bf16[4,32,128]{2,1,0:T(8,128)(2,1)S(1)}, u32[]{:S(2)}, u32[]{:S(2)}) collective-permute-start(bf16[4,32,128]{2,1,0:T(8,128)(2,1)S(1)} %get-tuple-element.633), channel_id=1, source_target_pairs={{0,1},{1,2},{2,3},{3,4},{4,5},{5,6},{6,7},{7,0},{8,9},{9,10},{10,1... | collective-permute-start | bytes 98312 | tf_op jit(solution)/shard_map/while/body/eval_jaxpr/ppermute | solution.py:63
  52.8 1.0 collective-permute-done.1
  53.9 3.1 %convolution_bitcast_fusion.2 = f32[4,32,128]{2,1,0:T(8,128)} fusion(bf16[4,32,32,128]{3,2,1,0:T(8,128)(2,1)} %param.17, f32[4,32,32,32]{2,3,1,0:T(8,128)} %copy-done, f32[4,32,32]{2,1,0:T(8,128)S(1)} %log_add_fusion), kind=kOutput, calls=%fused_computation.50 | convolution fusion | flops 33816576 | bytes 1654784 | tf_op jit(solution)/shard_map/cril,crie->cle/dot_general | solution.py:81
  57.0 2.0 %fusion.27 = (f32[4,32,32]{2,1,0:T(8,128)S(1)}, bf16[4,32,32,128]{3,2,1,0:T(8,128)(2,1)}) fusion(bf16[4,32,32,128]{3,2,1,0:T(8,128)(2,1)S(1)} %copy-done.3, f32[4,32,32,128]{3,2,1,0:T(8,128)S(1)} %get-tuple-element.406, f32[4,32,32]{2,1,0:T(8,128)S(1)} %get-tuple-element.407), kind=kLoop, calls=%fused_computation.37 | loop fusion | flops 3141632 | bytes 4227072 | tf_op jit(solution)/shard_map/bqhd,bqhd->bqh/dot_general | solution.py:71
  59.0 1.8 %multiply_convert_fusion.1 = bf16[4,32,32,32]{2,3,1,0:T(8,128)(2,1)S(1)} fusion(f32[4,32,32,32]{2,3,1,0:T(8,128)S(1)} %copy-done.1, bf16[4,32,32,128]{3,2,1,0:T(8,128)(2,1)S(1)} %copy-done.3, f32[4,32,32]{2,1,0:T(8,128)S(1)} %get-tuple-element.659, f32[4,32,32]{2,1,0:T(8,128)S(1)} %log_add_fusion, bf16[4,32,128]{2,1,0:T(8,128)(2,1)S(1)} %copy.107), kind=kOutput, calls=%fused_computation.39 | convolution fusion | flops 34078720 | bytes 1900544 | tf_op jit(solution)/shard_map/crie,cle->cril/dot_general | solution.py:77
  60.8 1.2 fusion.31
  62.5 1.4 copy.21
  63.9 1.4 copy.22
  65.3 79.0 %while.43 = (s32[]{:T(128)}, bf16[4,32,128]{2,1,0:T(8,128)(2,1)S(1)}, bf16[4,32,128]{2,1,0:T(8,128)(2,1)S(1)}, f32[4,32,32,128]{3,2,1,0:T(8,128)S(1)}, f32[4,32,...) while((s32[]{:T(128)}, ...), condition=%wide.region_11.12_spmd, body=%wide.region_8.11_spmd.sunk | while | flops 169918464 | bytes 16531903 | solution.py:93
  65.3 2.3 %collective-permute-start.4 = (f32[4,32,128]{2,1,0:T(8,128)}, f32[4,32,128]{2,1,0:T(8,128)S(1)}, u32[]{:S(2)}, u32[]{:S(2)}) collective-permute-start(f32[4,32,128]{2,1,0:T(8,128)} %get-tuple-element.665), channel_id=1, source_target_pairs={{0,1},{1,2},{2,3},{3,4},{4,5},{5,6},{6,7},{7,0},{8,9},{9,10},{10,1... | collective-permute-start | bytes 196616 | tf_op jit(solution)/shard_map/while/body/eval_jaxpr/ppermute | solution.py:89
  68.0 6.0 %collective-permute-start.3 = (bf16[4,32,128]{2,1,0:T(8,128)(2,1)S(1)}, bf16[4,32,128]{2,1,0:T(8,128)(2,1)S(1)}, u32[]{:S(2)}, u32[]{:S(2)}) collective-permute-start(bf16[4,32,128]{2,1,0:T(8,128)(2,1)S(1)} %get-tuple-element.663), channel_id=1, source_target_pairs={{0,1},{1,2},{2,3},{3,4},{4,5},{5,6},{6,7},{7,0},{8,9},{9,10},{10,1... | collective-permute-start | bytes 98312 | tf_op jit(solution)/shard_map/while/body/eval_jaxpr/ppermute | solution.py:89
  75.5 5.5 %conditional.5 = ((f32[4,32,32,128]{3,2,1,0:T(8,128)S(1)}, f32[4,32,128]{2,1,0:T(8,128)S(1)}, f32[4,32,128]{2,1,0:T(8,128)S(1)})) conditional(s32[]{:T(128)} %convert_element_type.102, (f32[4,32,32,128]{3,2,1,0:T(8,128)S(1)}, f32[4,32,128]{2,1,0:T(8,128)S(1)}, f32[4,32,128]{2,1,0:T(8,128)S(1)}) %tuple.87, (bf16[4,32,32,128]{3,1,2,0:T(8,128)(2,1)S(1)}, ...), branch_computations={%region_9.9_spmd, %region_10.10_spmd} | conditional | flops 169918464 | bytes 15351868 | solution.py:90
  76.8 1.3 multiply_convert_fusion
  79.2 1.8 %fusion.12 = f32[4,32,128]{2,1,0:T(8,128)S(1)} fusion(f32[4,32,128]{2,1,0:T(8,128)S(1)} %get-tuple-element.380, f32[4,32,32,32]{3,2,1,0:T(8,128)S(1)} %fusion.19, f32[4,32,32]{2,1,0:T(8,128)S(1)} %get-tuple-element.375, bf16[4,32,32,128]{3,1,2,0:T(8,128)(2,1)S(1)} %copy-done.5), kind=kOutput, calls=%fused_computation.21 | convolution fusion | flops 33964032 | bytes 1720320 | tf_op jit(solution)/shard_map/while/body/eval_jaxpr/cond/branch_1_fun/cril,crie->cle/dot_general | solution.py:81
  82.3 2.3 %collective-permute-start.4 = (f32[4,32,128]{2,1,0:T(8,128)}, f32[4,32,128]{2,1,0:T(8,128)S(1)}, u32[]{:S(2)}, u32[]{:S(2)}) collective-permute-start(f32[4,32,128]{2,1,0:T(8,128)} %get-tuple-element.665), channel_id=1, source_target_pairs={{0,1},{1,2},{2,3},{3,4},{4,5},{5,6},{6,7},{7,0},{8,9},{9,10},{10,1... | collective-permute-start | bytes 196616 | tf_op jit(solution)/shard_map/while/body/eval_jaxpr/ppermute | solution.py:89
  84.6 1.5 collective-permute-start.5
  86.0 2.3 %collective-permute-start.3 = (bf16[4,32,128]{2,1,0:T(8,128)(2,1)S(1)}, bf16[4,32,128]{2,1,0:T(8,128)(2,1)S(1)}, u32[]{:S(2)}, u32[]{:S(2)}) collective-permute-start(bf16[4,32,128]{2,1,0:T(8,128)(2,1)S(1)} %get-tuple-element.663), channel_id=1, source_target_pairs={{0,1},{1,2},{2,3},{3,4},{4,5},{5,6},{6,7},{7,0},{8,9},{9,10},{10,1... | collective-permute-start | bytes 98312 | tf_op jit(solution)/shard_map/while/body/eval_jaxpr/ppermute | solution.py:89
  90.9 7.8 %collective-permute-start.4 = (f32[4,32,128]{2,1,0:T(8,128)}, f32[4,32,128]{2,1,0:T(8,128)S(1)}, u32[]{:S(2)}, u32[]{:S(2)}) collective-permute-start(f32[4,32,128]{2,1,0:T(8,128)} %get-tuple-element.665), channel_id=1, source_target_pairs={{0,1},{1,2},{2,3},{3,4},{4,5},{5,6},{6,7},{7,0},{8,9},{9,10},{10,1... | collective-permute-start | bytes 196616 | tf_op jit(solution)/shard_map/while/body/eval_jaxpr/ppermute | solution.py:89
  98.8 1.4 collective-permute-start.3
  102.8 2.4 %collective-permute-start.4 = (f32[4,32,128]{2,1,0:T(8,128)}, f32[4,32,128]{2,1,0:T(8,128)S(1)}, u32[]{:S(2)}, u32[]{:S(2)}) collective-permute-start(f32[4,32,128]{2,1,0:T(8,128)} %get-tuple-element.665), channel_id=1, source_target_pairs={{0,1},{1,2},{2,3},{3,4},{4,5},{5,6},{6,7},{7,0},{8,9},{9,10},{10,1... | collective-permute-start | bytes 196616 | tf_op jit(solution)/shard_map/while/body/eval_jaxpr/ppermute | solution.py:89
  105.1 4.4 %collective-permute-start.5 = (f32[4,32,128]{2,1,0:T(8,128)}, f32[4,32,128]{2,1,0:T(8,128)S(1)}, u32[]{:S(2)}, u32[]{:S(2)}) collective-permute-start(f32[4,32,128]{2,1,0:T(8,128)} %get-tuple-element.666), channel_id=1, source_target_pairs={{0,1},{1,2},{2,3},{3,4},{4,5},{5,6},{6,7},{7,0},{8,9},{9,10},{10,1... | collective-permute-start | bytes 196616 | tf_op jit(solution)/shard_map/while/body/eval_jaxpr/ppermute | solution.py:89
  109.5 2.5 %collective-permute-start.3 = (bf16[4,32,128]{2,1,0:T(8,128)(2,1)S(1)}, bf16[4,32,128]{2,1,0:T(8,128)(2,1)S(1)}, u32[]{:S(2)}, u32[]{:S(2)}) collective-permute-start(bf16[4,32,128]{2,1,0:T(8,128)(2,1)S(1)} %get-tuple-element.663), channel_id=1, source_target_pairs={{0,1},{1,2},{2,3},{3,4},{4,5},{5,6},{6,7},{7,0},{8,9},{9,10},{10,1... | collective-permute-start | bytes 98312 | tf_op jit(solution)/shard_map/while/body/eval_jaxpr/ppermute | solution.py:89
  114.6 2.4 %collective-permute-start.4 = (f32[4,32,128]{2,1,0:T(8,128)}, f32[4,32,128]{2,1,0:T(8,128)S(1)}, u32[]{:S(2)}, u32[]{:S(2)}) collective-permute-start(f32[4,32,128]{2,1,0:T(8,128)} %get-tuple-element.665), channel_id=1, source_target_pairs={{0,1},{1,2},{2,3},{3,4},{4,5},{5,6},{6,7},{7,0},{8,9},{9,10},{10,1... | collective-permute-start | bytes 196616 | tf_op jit(solution)/shard_map/while/body/eval_jaxpr/ppermute | solution.py:89
  117.0 6.8 %collective-permute-start.3 = (bf16[4,32,128]{2,1,0:T(8,128)(2,1)S(1)}, bf16[4,32,128]{2,1,0:T(8,128)(2,1)S(1)}, u32[]{:S(2)}, u32[]{:S(2)}) collective-permute-start(bf16[4,32,128]{2,1,0:T(8,128)(2,1)S(1)} %get-tuple-element.663), channel_id=1, source_target_pairs={{0,1},{1,2},{2,3},{3,4},{4,5},{5,6},{6,7},{7,0},{8,9},{9,10},{10,1... | collective-permute-start | bytes 98312 | tf_op jit(solution)/shard_map/while/body/eval_jaxpr/ppermute | solution.py:89
  126.4 2.4 %collective-permute-start.4 = (f32[4,32,128]{2,1,0:T(8,128)}, f32[4,32,128]{2,1,0:T(8,128)S(1)}, u32[]{:S(2)}, u32[]{:S(2)}) collective-permute-start(f32[4,32,128]{2,1,0:T(8,128)} %get-tuple-element.665), channel_id=1, source_target_pairs={{0,1},{1,2},{2,3},{3,4},{4,5},{5,6},{6,7},{7,0},{8,9},{9,10},{10,1... | collective-permute-start | bytes 196616 | tf_op jit(solution)/shard_map/while/body/eval_jaxpr/ppermute | solution.py:89
  128.8 1.4 collective-permute-start.3
  130.2 4.0 %collective-permute-start.2 = (bf16[4,32,128]{2,1,0:T(8,128)(2,1)S(1)}, bf16[4,32,128]{2,1,0:T(8,128)(2,1)S(1)}, u32[]{:S(2)}, u32[]{:S(2)}) collective-permute-start(bf16[4,32,128]{2,1,0:T(8,128)(2,1)S(1)} %get-tuple-element.662), channel_id=1, source_target_pairs={{0,1},{1,2},{2,3},{3,4},{4,5},{5,6},{6,7},{7,0},{8,9},{9,10},{10,1... | collective-permute-start | bytes 98312 | tf_op jit(solution)/shard_map/while/body/eval_jaxpr/ppermute | solution.py:89
  134.2 1.0 collective-permute-done.2
  136.5 2.3 %collective-permute-start.4 = (f32[4,32,128]{2,1,0:T(8,128)}, f32[4,32,128]{2,1,0:T(8,128)S(1)}, u32[]{:S(2)}, u32[]{:S(2)}) collective-permute-start(f32[4,32,128]{2,1,0:T(8,128)} %get-tuple-element.665), channel_id=1, source_target_pairs={{0,1},{1,2},{2,3},{3,4},{4,5},{5,6},{6,7},{7,0},{8,9},{9,10},{10,1... | collective-permute-start | bytes 196616 | tf_op jit(solution)/shard_map/while/body/eval_jaxpr/ppermute | solution.py:89
  139.3 2.4 %collective-permute-start.3 = (bf16[4,32,128]{2,1,0:T(8,128)(2,1)S(1)}, bf16[4,32,128]{2,1,0:T(8,128)(2,1)S(1)}, u32[]{:S(2)}, u32[]{:S(2)}) collective-permute-start(bf16[4,32,128]{2,1,0:T(8,128)(2,1)S(1)} %get-tuple-element.663), channel_id=1, source_target_pairs={{0,1},{1,2},{2,3},{3,4},{4,5},{5,6},{6,7},{7,0},{8,9},{9,10},{10,1... | collective-permute-start | bytes 98312 | tf_op jit(solution)/shard_map/while/body/eval_jaxpr/ppermute | solution.py:89
  144.3 6.4 %collective-permute-start.6 = (f32[4,32,128]{2,1,0:T(8,128)}, f32[4,32,128]{2,1,0:T(8,128)S(1)}, u32[]{:S(2)}, u32[]{:S(2)}) collective-permute-start(f32[4,32,128]{2,1,0:T(8,128)} %get-tuple-element.410), channel_id=1, source_target_pairs={{0,1},{1,2},{2,3},{3,4},{4,5},{5,6},{6,7},{7,0},{8,9},{9,10},{10,1... | collective-permute-start | bytes 196616 | tf_op jit(solution)/shard_map/ppermute | solution.py:94
  152.8 1.7 %fusion.26 = bf16[4,32,32,128]{3,2,1,0:T(8,128)(2,1)} fusion(f32[4,32,32,64]{3,2,1,0:T(8,128)S(1)} %get-tuple-element.468, f32[4,32,32,64]{3,2,1,0:T(8,128)S(1)} %get-tuple-element.467, f32[4,32,32,128]{3,2,1,0:T(8,128)S(1)} %get-tuple-element.409, f32[32,128]{1,0:T(8,128)S(1)} %copy-done.10, f32[32,128]{1,0:T(8,128)S(1)} %get-tuple-element.479), kind=kLoop, calls=%fused_computation.35 | loop fusion | flops 2621440 | bytes 5275648 | tf_op jit(solution)/shard_map/convert_element_type | solution.py:95
  (160 shorter events, 36.6 us)
Async XLA Ops:
  2.9 2.1 %copy-start.9 = (bf16[4,32,128]{2,1,0:T(8,128)(2,1)S(1)}, bf16[4,32,128]{2,1,0:T(8,128)(2,1)}, u32[]{:S(2)}) copy-start(bf16[4,32,128]{2,1,0:T(8,128)(2,1)} %param.14) | copy-start | bytes 98308
  2.9 2.3 %copy-start.4 = (bf16[4,32,32,128]{3,2,1,0:T(8,128)(2,1)S(1)}, bf16[4,32,32,128]{3,2,1,0:T(8,128)(2,1)}, u32[]{:S(2)}) copy-start(bf16[4,32,32,128]{3,2,1,0:T(8,128)(2,1)} %param.13) | copy-start | bytes 3145732
  10.4 3.7 %collective-permute-start = (bf16[4,32,128]{2,1,0:T(8,128)(2,1)S(1)}, bf16[4,32,128]{2,1,0:T(8,128)(2,1)S(1)}, u32[]{:S(2)}, u32[]{:S(2)}) collective-permute-start(bf16[4,32,128]{2,1,0:T(8,128)(2,1)S(1)} %get-tuple-element.632), channel_id=1, source_target_pairs={{0,1},{1,2},{2,3},{3,4},{4,5},{5,6},{6,7},{7,0},{8,9},{9,10},{10,1... | collective-permute-start | bytes 98312 | tf_op jit(solution)/shard_map/while/body/eval_jaxpr/ppermute | solution.py:63
  13.1 1.3 collective-permute-start.1
  18.3 3.4 %collective-permute-start = (bf16[4,32,128]{2,1,0:T(8,128)(2,1)S(1)}, bf16[4,32,128]{2,1,0:T(8,128)(2,1)S(1)}, u32[]{:S(2)}, u32[]{:S(2)}) collective-permute-start(bf16[4,32,128]{2,1,0:T(8,128)(2,1)S(1)} %get-tuple-element.632), channel_id=1, source_target_pairs={{0,1},{1,2},{2,3},{3,4},{4,5},{5,6},{6,7},{7,0},{8,9},{9,10},{10,1... | collective-permute-start | bytes 98312 | tf_op jit(solution)/shard_map/while/body/eval_jaxpr/ppermute | solution.py:63
  20.7 1.3 collective-permute-start.1
  22.0 7.2 %collective-permute-start = (bf16[4,32,128]{2,1,0:T(8,128)(2,1)S(1)}, bf16[4,32,128]{2,1,0:T(8,128)(2,1)S(1)}, u32[]{:S(2)}, u32[]{:S(2)}) collective-permute-start(bf16[4,32,128]{2,1,0:T(8,128)(2,1)S(1)} %get-tuple-element.632), channel_id=1, source_target_pairs={{0,1},{1,2},{2,3},{3,4},{4,5},{5,6},{6,7},{7,0},{8,9},{9,10},{10,1... | collective-permute-start | bytes 98312 | tf_op jit(solution)/shard_map/while/body/eval_jaxpr/ppermute | solution.py:63
  28.2 1.3 collective-permute-start.1
  29.6 5.6 %collective-permute-start = (bf16[4,32,128]{2,1,0:T(8,128)(2,1)S(1)}, bf16[4,32,128]{2,1,0:T(8,128)(2,1)S(1)}, u32[]{:S(2)}, u32[]{:S(2)}) collective-permute-start(bf16[4,32,128]{2,1,0:T(8,128)(2,1)S(1)} %get-tuple-element.632), channel_id=1, source_target_pairs={{0,1},{1,2},{2,3},{3,4},{4,5},{5,6},{6,7},{7,0},{8,9},{9,10},{10,1... | collective-permute-start | bytes 98312 | tf_op jit(solution)/shard_map/while/body/eval_jaxpr/ppermute | solution.py:63
  32.0 4.2 %collective-permute-start.1 = (bf16[4,32,128]{2,1,0:T(8,128)(2,1)S(1)}, bf16[4,32,128]{2,1,0:T(8,128)(2,1)S(1)}, u32[]{:S(2)}, u32[]{:S(2)}) collective-permute-start(bf16[4,32,128]{2,1,0:T(8,128)(2,1)S(1)} %get-tuple-element.633), channel_id=1, source_target_pairs={{0,1},{1,2},{2,3},{3,4},{4,5},{5,6},{6,7},{7,0},{8,9},{9,10},{10,1... | collective-permute-start | bytes 98312 | tf_op jit(solution)/shard_map/while/body/eval_jaxpr/ppermute | solution.py:63
  36.2 3.4 %collective-permute-start = (bf16[4,32,128]{2,1,0:T(8,128)(2,1)S(1)}, bf16[4,32,128]{2,1,0:T(8,128)(2,1)S(1)}, u32[]{:S(2)}, u32[]{:S(2)}) collective-permute-start(bf16[4,32,128]{2,1,0:T(8,128)(2,1)S(1)} %get-tuple-element.632), channel_id=1, source_target_pairs={{0,1},{1,2},{2,3},{3,4},{4,5},{5,6},{6,7},{7,0},{8,9},{9,10},{10,1... | collective-permute-start | bytes 98312 | tf_op jit(solution)/shard_map/while/body/eval_jaxpr/ppermute | solution.py:63
  38.6 1.4 collective-permute-start.1
  40.0 7.1 %collective-permute-start = (bf16[4,32,128]{2,1,0:T(8,128)(2,1)S(1)}, bf16[4,32,128]{2,1,0:T(8,128)(2,1)S(1)}, u32[]{:S(2)}, u32[]{:S(2)}) collective-permute-start(bf16[4,32,128]{2,1,0:T(8,128)(2,1)S(1)} %get-tuple-element.632), channel_id=1, source_target_pairs={{0,1},{1,2},{2,3},{3,4},{4,5},{5,6},{6,7},{7,0},{8,9},{9,10},{10,1... | collective-permute-start | bytes 98312 | tf_op jit(solution)/shard_map/while/body/eval_jaxpr/ppermute | solution.py:63
  46.0 1.5 collective-permute-start.1
  47.5 5.3 %collective-permute-start = (bf16[4,32,128]{2,1,0:T(8,128)(2,1)S(1)}, bf16[4,32,128]{2,1,0:T(8,128)(2,1)S(1)}, u32[]{:S(2)}, u32[]{:S(2)}) collective-permute-start(bf16[4,32,128]{2,1,0:T(8,128)(2,1)S(1)} %get-tuple-element.632), channel_id=1, source_target_pairs={{0,1},{1,2},{2,3},{3,4},{4,5},{5,6},{6,7},{7,0},{8,9},{9,10},{10,1... | collective-permute-start | bytes 98312 | tf_op jit(solution)/shard_map/while/body/eval_jaxpr/ppermute | solution.py:63
  49.9 3.9 %collective-permute-start.1 = (bf16[4,32,128]{2,1,0:T(8,128)(2,1)S(1)}, bf16[4,32,128]{2,1,0:T(8,128)(2,1)S(1)}, u32[]{:S(2)}, u32[]{:S(2)}) collective-permute-start(bf16[4,32,128]{2,1,0:T(8,128)(2,1)S(1)} %get-tuple-element.633), channel_id=1, source_target_pairs={{0,1},{1,2},{2,3},{3,4},{4,5},{5,6},{6,7},{7,0},{8,9},{9,10},{10,1... | collective-permute-start | bytes 98312 | tf_op jit(solution)/shard_map/while/body/eval_jaxpr/ppermute | solution.py:63
  53.8 3.1 %copy-start.3 = (bf16[4,32,32,128]{3,2,1,0:T(8,128)(2,1)S(1)}, bf16[4,32,32,128]{3,2,1,0:T(8,128)(2,1)}, u32[]{:S(2)}) copy-start(bf16[4,32,32,128]{3,2,1,0:T(8,128)(2,1)} %param.17) | copy-start | bytes 3145732
  57.0 2.0 %copy-start.1 = (f32[4,32,32,32]{2,3,1,0:T(8,128)S(1)}, f32[4,32,32,32]{2,3,1,0:T(8,128)}, u32[]{:S(2)}) copy-start(f32[4,32,32,32]{2,3,1,0:T(8,128)} %copy-done) | copy-start | bytes 1572868
  65.3 10.2 %collective-permute-start.4 = (f32[4,32,128]{2,1,0:T(8,128)}, f32[4,32,128]{2,1,0:T(8,128)S(1)}, u32[]{:S(2)}, u32[]{:S(2)}) collective-permute-start(f32[4,32,128]{2,1,0:T(8,128)} %get-tuple-element.665), channel_id=1, source_target_pairs={{0,1},{1,2},{2,3},{3,4},{4,5},{5,6},{6,7},{7,0},{8,9},{9,10},{10,1... | collective-permute-start | bytes 196616 | tf_op jit(solution)/shard_map/while/body/eval_jaxpr/ppermute | solution.py:89
  67.7 7.9 %collective-permute-start.5 = (f32[4,32,128]{2,1,0:T(8,128)}, f32[4,32,128]{2,1,0:T(8,128)S(1)}, u32[]{:S(2)}, u32[]{:S(2)}) collective-permute-start(f32[4,32,128]{2,1,0:T(8,128)} %get-tuple-element.666), channel_id=1, source_target_pairs={{0,1},{1,2},{2,3},{3,4},{4,5},{5,6},{6,7},{7,0},{8,9},{9,10},{10,1... | collective-permute-start | bytes 196616 | tf_op jit(solution)/shard_map/while/body/eval_jaxpr/ppermute | solution.py:89
  68.0 7.0 %collective-permute-start.3 = (bf16[4,32,128]{2,1,0:T(8,128)(2,1)S(1)}, bf16[4,32,128]{2,1,0:T(8,128)(2,1)S(1)}, u32[]{:S(2)}, u32[]{:S(2)}) collective-permute-start(bf16[4,32,128]{2,1,0:T(8,128)(2,1)S(1)} %get-tuple-element.663), channel_id=1, source_target_pairs={{0,1},{1,2},{2,3},{3,4},{4,5},{5,6},{6,7},{7,0},{8,9},{9,10},{10,1... | collective-permute-start | bytes 98312 | tf_op jit(solution)/shard_map/while/body/eval_jaxpr/ppermute | solution.py:89
  74.0 1.5 collective-permute-start.2
  82.3 7.4 %collective-permute-start.4 = (f32[4,32,128]{2,1,0:T(8,128)}, f32[4,32,128]{2,1,0:T(8,128)S(1)}, u32[]{:S(2)}, u32[]{:S(2)}) collective-permute-start(f32[4,32,128]{2,1,0:T(8,128)} %get-tuple-element.665), channel_id=1, source_target_pairs={{0,1},{1,2},{2,3},{3,4},{4,5},{5,6},{6,7},{7,0},{8,9},{9,10},{10,1... | collective-permute-start | bytes 196616 | tf_op jit(solution)/shard_map/while/body/eval_jaxpr/ppermute | solution.py:89
  84.6 5.1 %collective-permute-start.5 = (f32[4,32,128]{2,1,0:T(8,128)}, f32[4,32,128]{2,1,0:T(8,128)S(1)}, u32[]{:S(2)}, u32[]{:S(2)}) collective-permute-start(f32[4,32,128]{2,1,0:T(8,128)} %get-tuple-element.666), channel_id=1, source_target_pairs={{0,1},{1,2},{2,3},{3,4},{4,5},{5,6},{6,7},{7,0},{8,9},{9,10},{10,1... | collective-permute-start | bytes 196616 | tf_op jit(solution)/shard_map/while/body/eval_jaxpr/ppermute | solution.py:89
  86.0 3.3 %collective-permute-start.3 = (bf16[4,32,128]{2,1,0:T(8,128)(2,1)S(1)}, bf16[4,32,128]{2,1,0:T(8,128)(2,1)S(1)}, u32[]{:S(2)}, u32[]{:S(2)}) collective-permute-start(bf16[4,32,128]{2,1,0:T(8,128)(2,1)S(1)} %get-tuple-element.663), channel_id=1, source_target_pairs={{0,1},{1,2},{2,3},{3,4},{4,5},{5,6},{6,7},{7,0},{8,9},{9,10},{10,1... | collective-permute-start | bytes 98312 | tf_op jit(solution)/shard_map/while/body/eval_jaxpr/ppermute | solution.py:89
  88.3 1.3 collective-permute-start.2
  90.9 10.6 %collective-permute-start.4 = (f32[4,32,128]{2,1,0:T(8,128)}, f32[4,32,128]{2,1,0:T(8,128)S(1)}, u32[]{:S(2)}, u32[]{:S(2)}) collective-permute-start(f32[4,32,128]{2,1,0:T(8,128)} %get-tuple-element.665), channel_id=1, source_target_pairs={{0,1},{1,2},{2,3},{3,4},{4,5},{5,6},{6,7},{7,0},{8,9},{9,10},{10,1... | collective-permute-start | bytes 196616 | tf_op jit(solution)/shard_map/while/body/eval_jaxpr/ppermute | solution.py:89
  98.8 2.7 %collective-permute-start.5 = (f32[4,32,128]{2,1,0:T(8,128)}, f32[4,32,128]{2,1,0:T(8,128)S(1)}, u32[]{:S(2)}, u32[]{:S(2)}) collective-permute-start(f32[4,32,128]{2,1,0:T(8,128)} %get-tuple-element.666), channel_id=1, source_target_pairs={{0,1},{1,2},{2,3},{3,4},{4,5},{5,6},{6,7},{7,0},{8,9},{9,10},{10,1... | collective-permute-start | bytes 196616 | tf_op jit(solution)/shard_map/while/body/eval_jaxpr/ppermute | solution.py:89
  98.8 2.4 %collective-permute-start.3 = (bf16[4,32,128]{2,1,0:T(8,128)(2,1)S(1)}, bf16[4,32,128]{2,1,0:T(8,128)(2,1)S(1)}, u32[]{:S(2)}, u32[]{:S(2)}) collective-permute-start(bf16[4,32,128]{2,1,0:T(8,128)(2,1)S(1)} %get-tuple-element.663), channel_id=1, source_target_pairs={{0,1},{1,2},{2,3},{3,4},{4,5},{5,6},{6,7},{7,0},{8,9},{9,10},{10,1... | collective-permute-start | bytes 98312 | tf_op jit(solution)/shard_map/while/body/eval_jaxpr/ppermute | solution.py:89
  100.2 1.3 collective-permute-start.2
  102.8 10.6 %collective-permute-start.4 = (f32[4,32,128]{2,1,0:T(8,128)}, f32[4,32,128]{2,1,0:T(8,128)S(1)}, u32[]{:S(2)}, u32[]{:S(2)}) collective-permute-start(f32[4,32,128]{2,1,0:T(8,128)} %get-tuple-element.665), channel_id=1, source_target_pairs={{0,1},{1,2},{2,3},{3,4},{4,5},{5,6},{6,7},{7,0},{8,9},{9,10},{10,1... | collective-permute-start | bytes 196616 | tf_op jit(solution)/shard_map/while/body/eval_jaxpr/ppermute | solution.py:89
  105.1 8.2 %collective-permute-start.5 = (f32[4,32,128]{2,1,0:T(8,128)}, f32[4,32,128]{2,1,0:T(8,128)S(1)}, u32[]{:S(2)}, u32[]{:S(2)}) collective-permute-start(f32[4,32,128]{2,1,0:T(8,128)} %get-tuple-element.666), channel_id=1, source_target_pairs={{0,1},{1,2},{2,3},{3,4},{4,5},{5,6},{6,7},{7,0},{8,9},{9,10},{10,1... | collective-permute-start | bytes 196616 | tf_op jit(solution)/shard_map/while/body/eval_jaxpr/ppermute | solution.py:89
  109.5 3.5 %collective-permute-start.3 = (bf16[4,32,128]{2,1,0:T(8,128)(2,1)S(1)}, bf16[4,32,128]{2,1,0:T(8,128)(2,1)S(1)}, u32[]{:S(2)}, u32[]{:S(2)}) collective-permute-start(bf16[4,32,128]{2,1,0:T(8,128)(2,1)S(1)} %get-tuple-element.663), channel_id=1, source_target_pairs={{0,1},{1,2},{2,3},{3,4},{4,5},{5,6},{6,7},{7,0},{8,9},{9,10},{10,1... | collective-permute-start | bytes 98312 | tf_op jit(solution)/shard_map/while/body/eval_jaxpr/ppermute | solution.py:89
  112.0 1.3 collective-permute-start.2
  114.6 10.6 %collective-permute-start.4 = (f32[4,32,128]{2,1,0:T(8,128)}, f32[4,32,128]{2,1,0:T(8,128)S(1)}, u32[]{:S(2)}, u32[]{:S(2)}) collective-permute-start(f32[4,32,128]{2,1,0:T(8,128)} %get-tuple-element.665), channel_id=1, source_target_pairs={{0,1},{1,2},{2,3},{3,4},{4,5},{5,6},{6,7},{7,0},{8,9},{9,10},{10,1... | collective-permute-start | bytes 196616 | tf_op jit(solution)/shard_map/while/body/eval_jaxpr/ppermute | solution.py:89
  117.0 8.2 %collective-permute-start.5 = (f32[4,32,128]{2,1,0:T(8,128)}, f32[4,32,128]{2,1,0:T(8,128)S(1)}, u32[]{:S(2)}, u32[]{:S(2)}) collective-permute-start(f32[4,32,128]{2,1,0:T(8,128)} %get-tuple-element.666), channel_id=1, source_target_pairs={{0,1},{1,2},{2,3},{3,4},{4,5},{5,6},{6,7},{7,0},{8,9},{9,10},{10,1... | collective-permute-start | bytes 196616 | tf_op jit(solution)/shard_map/while/body/eval_jaxpr/ppermute | solution.py:89
  117.0 7.9 %collective-permute-start.3 = (bf16[4,32,128]{2,1,0:T(8,128)(2,1)S(1)}, bf16[4,32,128]{2,1,0:T(8,128)(2,1)S(1)}, u32[]{:S(2)}, u32[]{:S(2)}) collective-permute-start(bf16[4,32,128]{2,1,0:T(8,128)(2,1)S(1)} %get-tuple-element.663), channel_id=1, source_target_pairs={{0,1},{1,2},{2,3},{3,4},{4,5},{5,6},{6,7},{7,0},{8,9},{9,10},{10,1... | collective-permute-start | bytes 98312 | tf_op jit(solution)/shard_map/while/body/eval_jaxpr/ppermute | solution.py:89
  123.8 1.3 collective-permute-start.2
  126.4 8.8 %collective-permute-start.4 = (f32[4,32,128]{2,1,0:T(8,128)}, f32[4,32,128]{2,1,0:T(8,128)S(1)}, u32[]{:S(2)}, u32[]{:S(2)}) collective-permute-start(f32[4,32,128]{2,1,0:T(8,128)} %get-tuple-element.665), channel_id=1, source_target_pairs={{0,1},{1,2},{2,3},{3,4},{4,5},{5,6},{6,7},{7,0},{8,9},{9,10},{10,1... | collective-permute-start | bytes 196616 | tf_op jit(solution)/shard_map/while/body/eval_jaxpr/ppermute | solution.py:89
  128.8 6.4 %collective-permute-start.5 = (f32[4,32,128]{2,1,0:T(8,128)}, f32[4,32,128]{2,1,0:T(8,128)S(1)}, u32[]{:S(2)}, u32[]{:S(2)}) collective-permute-start(f32[4,32,128]{2,1,0:T(8,128)} %get-tuple-element.666), channel_id=1, source_target_pairs={{0,1},{1,2},{2,3},{3,4},{4,5},{5,6},{6,7},{7,0},{8,9},{9,10},{10,1... | collective-permute-start | bytes 196616 | tf_op jit(solution)/shard_map/while/body/eval_jaxpr/ppermute | solution.py:89
  128.8 5.4 %collective-permute-start.3 = (bf16[4,32,128]{2,1,0:T(8,128)(2,1)S(1)}, bf16[4,32,128]{2,1,0:T(8,128)(2,1)S(1)}, u32[]{:S(2)}, u32[]{:S(2)}) collective-permute-start(bf16[4,32,128]{2,1,0:T(8,128)(2,1)S(1)} %get-tuple-element.663), channel_id=1, source_target_pairs={{0,1},{1,2},{2,3},{3,4},{4,5},{5,6},{6,7},{7,0},{8,9},{9,10},{10,1... | collective-permute-start | bytes 98312 | tf_op jit(solution)/shard_map/while/body/eval_jaxpr/ppermute | solution.py:89
  130.2 5.0 %collective-permute-start.2 = (bf16[4,32,128]{2,1,0:T(8,128)(2,1)S(1)}, bf16[4,32,128]{2,1,0:T(8,128)(2,1)S(1)}, u32[]{:S(2)}, u32[]{:S(2)}) collective-permute-start(bf16[4,32,128]{2,1,0:T(8,128)(2,1)S(1)} %get-tuple-element.662), channel_id=1, source_target_pairs={{0,1},{1,2},{2,3},{3,4},{4,5},{5,6},{6,7},{7,0},{8,9},{9,10},{10,1... | collective-permute-start | bytes 98312 | tf_op jit(solution)/shard_map/while/body/eval_jaxpr/ppermute | solution.py:89
  136.5 6.5 %collective-permute-start.4 = (f32[4,32,128]{2,1,0:T(8,128)}, f32[4,32,128]{2,1,0:T(8,128)S(1)}, u32[]{:S(2)}, u32[]{:S(2)}) collective-permute-start(f32[4,32,128]{2,1,0:T(8,128)} %get-tuple-element.665), channel_id=1, source_target_pairs={{0,1},{1,2},{2,3},{3,4},{4,5},{5,6},{6,7},{7,0},{8,9},{9,10},{10,1... | collective-permute-start | bytes 196616 | tf_op jit(solution)/shard_map/while/body/eval_jaxpr/ppermute | solution.py:89
  138.9 4.2 %collective-permute-start.5 = (f32[4,32,128]{2,1,0:T(8,128)}, f32[4,32,128]{2,1,0:T(8,128)S(1)}, u32[]{:S(2)}, u32[]{:S(2)}) collective-permute-start(f32[4,32,128]{2,1,0:T(8,128)} %get-tuple-element.666), channel_id=1, source_target_pairs={{0,1},{1,2},{2,3},{3,4},{4,5},{5,6},{6,7},{7,0},{8,9},{9,10},{10,1... | collective-permute-start | bytes 196616 | tf_op jit(solution)/shard_map/while/body/eval_jaxpr/ppermute | solution.py:89
  139.3 3.4 %collective-permute-start.3 = (bf16[4,32,128]{2,1,0:T(8,128)(2,1)S(1)}, bf16[4,32,128]{2,1,0:T(8,128)(2,1)S(1)}, u32[]{:S(2)}, u32[]{:S(2)}) collective-permute-start(bf16[4,32,128]{2,1,0:T(8,128)(2,1)S(1)} %get-tuple-element.663), channel_id=1, source_target_pairs={{0,1},{1,2},{2,3},{3,4},{4,5},{5,6},{6,7},{7,0},{8,9},{9,10},{10,1... | collective-permute-start | bytes 98312 | tf_op jit(solution)/shard_map/while/body/eval_jaxpr/ppermute | solution.py:89
  141.7 1.3 collective-permute-start.2
  144.3 10.2 %collective-permute-start.6 = (f32[4,32,128]{2,1,0:T(8,128)}, f32[4,32,128]{2,1,0:T(8,128)S(1)}, u32[]{:S(2)}, u32[]{:S(2)}) collective-permute-start(f32[4,32,128]{2,1,0:T(8,128)} %get-tuple-element.410), channel_id=1, source_target_pairs={{0,1},{1,2},{2,3},{3,4},{4,5},{5,6},{6,7},{7,0},{8,9},{9,10},{10,1... | collective-permute-start | bytes 196616 | tf_op jit(solution)/shard_map/ppermute | solution.py:94
  151.5 3.0 %collective-permute-start.7 = (bf16[4,32,128]{2,1,0:T(8,128)(2,1)S(1)}, bf16[4,32,128]{2,1,0:T(8,128)(2,1)S(1)}, u32[]{:S(2)}, u32[]{:S(2)}) collective-permute-start(bf16[4,32,128]{2,1,0:T(8,128)(2,1)S(1)} %convert.15), channel_id=1, source_target_pairs={{0,1},{1,2},{2,3},{3,4},{4,5},{5,6},{6,7},{7,0},{8,9},{9,10},{10,1... | collective-permute-start | bytes 98312 | tf_op jit(solution)/shard_map/ppermute | solution.py:94
  (7 other events, 7.9 us)
where the time goes:
time: 159 us; the launch traced here: 156 us
  starting transfers between devices  94.4 us (59%)
  matrix products  17.3 us (11%)
  waiting for transfers between devices  16.5 us (10%)
  local copies, waits for them, and re-layouts  14.3 us (9%)
  other arithmetic  12.1 us (8%)
    ppermute x28, starting transfers between devices, backward_step(): lax.ppermute((key_blk, value_blk, dkey_blk, dvalue_blk), 'cp', shift_pairs)  55.9 us
    ppermute x14, starting transfers between devices, forward_step(): key_blk, value_blk = lax.ppermute((key_blk, value_blk), 'cp', shift_pairs)  31.7 us
    while x42, local copies, waits for them, and re-layouts  8.79 us
    ppermute x28, waiting for transfers between devices, backward_step(): lax.ppermute((key_blk, value_blk, dkey_blk, dvalue_blk), 'cp', shift_pairs)  8.61 us
    ppermute x14, waiting for transfers between devices, forward_step(): key_blk, value_blk = lax.ppermute((key_blk, value_blk), 'cp', shift_pairs)  7.87 us
    ppermute x2, starting transfers between devices, per_device(): lax.ppermute((bwd_carry[3], bwd_carry[4]), 'cp', shift_pairs)  6.86 us
    dot_general x2, matrix products, backward_block(): jnp.einsum('cril,crie->cle', probs_f.astype(jnp.bfloat16), grad_out, pref...  4.86 us
    dot_general x3, matrix products, block_scores(): jnp.einsum('crie,cle->cril', query_rot, key_blk, preferred_element_type=j...  4.2 us
  transfers between devices with their start and end apart: 44, of which 25 were waited for; matrix products, arithmetic and copies ran while one was open for 2% of the time, Pallas kernels for 0%

commit v1 on v0

v1 whole, which is shorter than its diff:
```python
import functools

import jax
import jax.numpy as jnp
import numpy as np
from jax import lax
from jax.experimental import pallas as pl
from jax.experimental.pallas import tpu as pltpu
from jax.sharding import PartitionSpec as P

ROPE_BASE = 10000
CORES = 2
LOG2E = 1.4426950408889634
F32 = jnp.float32
BF16 = jnp.bfloat16
ROWS = 512


def dot_nn(a, b):
    return jnp.dot(a, b, preferred_element_type=F32)


def dot_nt(a, b):
    return lax.dot_general(a, b, (((1,), (1,)), ((), ())), preferred_element_type=F32)


def attend_kernel(cp, blk, q_hbm, g_hbm, k_hbm, v_hbm, pos_hbm, freq_hbm,
                  o_ref, dq_ref, rbuf, tabs_out,
                  k_ref, v_ref, pos_ref, freq_ref, qb, gb, rq, tabs, kvown, kvb, p_t, ds_t, part, osib, dqsib,
                  first_sem, loc_sem, qg_send, qg_recv, tab_send, tab_recv, kv_send, kv_recv,
                  r_send, r_recv, od_send, od_recv):
    chips = cp // CORES
    seqs = q_hbm.shape[0]
    mine = seqs // CORES
    rows, head = q_hbm.shape[1], q_hbm.shape[2]
    heads = rows // blk
    half_dim = head // 2
    keys = cp * blk
    scale = head ** -0.5
    me = lax.axis_index("cp")
    chip = lax.div(me, CORES)
    core = lax.rem(me, CORES)
    sib = chip * CORES + 1 - core

    def remote(src, dst, ssem, rsem, dev):
        return pltpu.make_async_remote_copy(src_ref=src, dst_ref=dst, send_sem=ssem, recv_sem=rsem,
                                            device_id={"cp": dev}, device_id_type=pl.DeviceIdType.MESH)

    first = [pltpu.make_async_copy(src, dst, first_sem.at[n]) for n, (src, dst) in enumerate(
        ((pos_hbm, pos_ref), (freq_hbm, freq_ref), (k_hbm, k_ref), (v_hbm, v_ref)))]
    for c in first:
        c.start()
    local = []
    for s in range(mine):
        local.append(pltpu.make_async_copy(q_hbm.at[core * mine + s], qb.at[s, 0], loc_sem.at[0, s]))
        local.append(pltpu.make_async_copy(g_hbm.at[core * mine + s], gb.at[s, 0], loc_sem.at[1, s]))
    for c in local:
        c.start()

    kvb[...] = jnp.zeros_like(kvb)
    rbuf[...] = jnp.zeros_like(rbuf)

    barrier = pltpu.get_barrier_semaphore()
    for d in range(1, cp):
        pl.semaphore_signal(barrier, inc=1, device_id={"cp": lax.rem(me + d, cp)},
                            device_id_type=pl.DeviceIdType.MESH)

    for c in first:
        c.wait()
    pos_row = jnp.broadcast_to(pos_ref[...].astype(F32), (blk, blk))
    ident = lax.broadcasted_iota(jnp.int32, (blk, blk), 0) == lax.broadcasted_iota(jnp.int32, (blk, blk), 1)
    pos_col = jnp.sum(jnp.where(ident, pos_row, 0.0), axis=1, keepdims=True)
    ang = pos_col * freq_ref[...]
    cos_t = jnp.cos(ang)
    lane = lax.broadcasted_iota(jnp.int32, (blk, head), 1)
    sin_t = jnp.where(lane < half_dim, -jnp.sin(ang), jnp.sin(ang))
    tabs[0, 0] = cos_t
    tabs[0, 1] = sin_t
    tabs_out[0] = cos_t
    tabs_out[1] = sin_t
    for b in range(seqs):
        kf = k_ref[b].astype(F32)
        kvown[b, 0] = (kf * cos_t + pltpu.roll(kf, half_dim, 1) * sin_t).astype(BF16)
        kvown[b, 1] = v_ref[b]

    pl.semaphore_wait(barrier, cp - 1)

    tab_copy = remote(tabs.at[0], tabs.at[1], tab_send, tab_recv, sib)
    tab_copy.start()

    def kv_copy(s, c2, k2):
        return remote(kvown.at[k2 * mine + s], kvb.at[s, me], kv_send.at[s, c2, k2], kv_recv.at[s, me],
                      c2 * CORES + k2)

    def kv_sib(s):
        return remote(kvown.at[(1 - core) * mine + s], kvb.at[s, me], kv_send.at[s, chip, 1 - core],
                      kv_recv.at[s, me], sib)

    def qg_copies(s):
        return (remote(q_hbm.at[(1 - core) * mine + s], qb.at[s, 1], qg_send.at[0, s], qg_recv.at[0, s], sib),
                remote(g_hbm.at[(1 - core) * mine + s], gb.at[s, 1], qg_send.at[1, s], qg_recv.at[1, s], sib))

    for s in range(mine):
        for c2 in range(chips):
            for k2 in range(CORES):
                @pl.when(c2 > chip)
                def _():
                    kv_copy(s, c2, k2).start()
        kv_sib(s).start()
        for c in qg_copies(s):
            c.start()
    for s in range(mine):
        kvb[s, me] = kvown[core * mine + s]

    def rope_q(s, h):
        x = qb[s, h].astype(F32)
        cos_q = jnp.broadcast_to(tabs[h, 0][:, None, :], (blk, heads, head)).reshape(rows, head)
        sin_q = jnp.broadcast_to(tabs[h, 1][:, None, :], (blk, heads, head)).reshape(rows, head)
        rq[s, h * rows:(h + 1) * rows, :] = (x * cos_q + pltpu.roll(x, half_dim, 1) * sin_q).astype(BF16)

    for c in local:
        c.wait()
    for s in range(mine):
        rope_q(s, 0)
    tab_copy.wait_recv()
    for s in range(mine):
        for c in qg_copies(s):
            c.wait_recv()
        rope_q(s, 1)

    def part_copy(s, x, c2, k2):
        return remote(part.at[s, c2 * CORES + k2, x], rbuf.at[chip, core * mine + s, x],
                      r_send.at[s, x, c2, k2], r_recv.at[chip, core * mine + s, x], c2 * CORES + k2)

    def part_sib(s, x):
        return remote(part.at[s, sib, x], rbuf.at[chip, core * mine + s, x],
                      r_send.at[s, x, chip, 1 - core], r_recv.at[chip, core * mine + s, x], sib)

    def send_part(s, x, val):
        part[s, :, x] = val.reshape(cp, blk, head)
        for c2 in range(chips):
            for k2 in range(CORES):
                @pl.when(c2 < chip)
                def _():
                    part_copy(s, x, c2, k2).start()
        part_sib(s, x).start()
        rbuf[chip, core * mine + s, x] = part[s, me, x]

    def out_copy(which, s):
        src, dst = ((osib, o_ref), (dqsib, dq_ref))[which]
        return remote(src.at[s], dst.at[core * mine + s], od_send.at[which, s], od_recv.at[which, s], sib)

    key_idx = lax.broadcasted_iota(jnp.int32, (keys, ROWS), 0)
    row_tok = lax.div(lax.broadcasted_iota(jnp.int32, (1, ROWS), 1), heads)

    for s in range(mine):
        for j in range(cp):
            @pl.when(jnp.logical_and(j < (chip + 1) * CORES, j != me))
            def _():
                pltpu.make_async_remote_copy(src_ref=kvown.at[s], dst_ref=kvb.at[s, j], send_sem=kv_send.at[s, 0, 0],
                                             recv_sem=kv_recv.at[s, j], device_id={"cp": sib},
                                             device_id_type=pl.DeviceIdType.MESH).wait_recv()
        kk = kvb[s, :, 0].reshape(keys, head)
        vv = kvb[s, :, 1].reshape(keys, head)
        v_t = vv.T
        for h in (1, 0):
            base = jnp.where(h == 0, me, sib) * blk
            for r in range(0, rows, ROWS):
                row0 = h * rows + r
                g = gb[s, h, r:r + ROWS, :]
                x = dot_nt(kk, rq[s, row0:row0 + ROWS, :])
                tok = row_tok + (base + r // heads)
                x = jnp.where(key_idx <= tok, x, -jnp.inf)
                mx = jnp.max(x, axis=0, keepdims=True)
                w = jnp.exp2((x - mx) * (scale * LOG2E))
                inv_l = 1.0 / jnp.sum(w, axis=0, keepdims=True)
                o_t = (dot_nn(v_t, w.astype(BF16)) * inv_l).astype(BF16)
                p = w * inv_l
                p_t[s, :, row0:row0 + ROWS] = p.astype(BF16)
                delta = jnp.sum(g.T.astype(F32) * o_t.astype(F32), axis=0, keepdims=True)
                dp = dot_nt(vv, g)
                ds_t[s, :, row0:row0 + ROWS] = (p * (dp - delta)).astype(BF16)
                if h == 0:
                    o_ref[core * mine + s, r:r + ROWS, :] = o_t.T
                else:
                    osib[s, r:r + ROWS, :] = o_t.T
            if h == 1:
                out_copy(0, s).start()
        send_part(s, 1, dot_nn(p_t[s], gb[s].reshape(CORES * rows, head)))
        send_part(s, 0, dot_nn(ds_t[s], rq[s]))

    for s in range(mine):
        k_t = kvb[s, :, 0].reshape(keys, head).T
        for h in (1, 0):
            for r in range(0, rows, ROWS):
                row0 = h * rows + r
                dqr = dot_nn(k_t, ds_t[s, :, row0:row0 + ROWS]).T * scale
                toks = ROWS // heads
                t0 = r // heads
                cos_q = jnp.broadcast_to(tabs[h, 0, t0:t0 + toks][:, None, :], (toks, heads, head)).reshape(ROWS, head)
                sin_q = jnp.broadcast_to(tabs[h, 1, t0:t0 + toks][:, None, :], (toks, heads, head)).reshape(ROWS, head)
                dq = (dqr * cos_q - pltpu.roll(dqr, half_dim, 1) * sin_q).astype(BF16)
                if h == 0:
                    dq_ref[core * mine + s, r:r + ROWS, :] = dq
                else:
                    dqsib[s, r:r + ROWS, :] = dq
            if h == 1:
                out_copy(1, s).start()

    for s in range(mine):
        for x in range(2):
            out_copy(x, s).wait()
            part_sib(s, x).wait_send()
            remote(part.at[s, sib, x], rbuf.at[chip, (1 - core) * mine + s, x], r_send.at[s, x, chip, 1 - core],
                   r_recv.at[chip, (1 - core) * mine + s, x], sib).wait_recv()
            for c2 in range(chips):
                for k2 in range(CORES):
                    @pl.when(c2 < chip)
                    def _():
                        part_copy(s, x, c2, k2).wait_send()

                    @pl.when(c2 > chip)
                    def _():
                        pltpu.make_async_remote_copy(
                            src_ref=part.at[s, 0, x], dst_ref=rbuf.at[c2, k2 * mine + s, x],
                            send_sem=r_send.at[s, x, 0, 0], recv_sem=r_recv.at[c2, k2 * mine + s, x],
                            device_id={"cp": sib}, device_id_type=pl.DeviceIdType.MESH).wait_recv()
        kv_sib(s).wait_send()
        for c in qg_copies(s):
            c.wait_send()
        for c2 in range(chips):
            for k2 in range(CORES):
                @pl.when(c2 > chip)
                def _():
                    kv_copy(s, c2, k2).wait_send()
    tab_copy.wait_send()


def finish_kernel(o_in, dq_in, rbuf, tabs, o_hbm, dq_hbm, dk_ref, dv_ref, sem):
    copies = [pltpu.make_async_copy(o_in, o_hbm, sem.at[0]), pltpu.make_async_copy(dq_in, dq_hbm, sem.at[1])]
    for c in copies:
        c.start()
    head = tabs.shape[-1]
    scale = head ** -0.5
    cos_t, sin_t = tabs[0], tabs[1]
    for b in range(dk_ref.shape[0]):
        dk = rbuf[0, b, 0]
        dv = rbuf[0, b, 1]
        for c in range(1, rbuf.shape[0]):
            dk = dk + rbuf[c, b, 0]
            dv = dv + rbuf[c, b, 1]
        dk = dk * scale
        dk_ref[b] = (dk * cos_t - pltpu.roll(dk, head // 2, 1) * sin_t).astype(BF16)
        dv_ref[b] = dv.astype(BF16)
    for c in copies:
        c.wait()


def solution(mesh):
    cp = mesh.shape["cp"]
    query_spec = P("dp", "cp", None, None)
    kv_spec = P("dp", "cp", None)
    pos_spec = P(("dp", "cp"))

    def per_device(query, key, value, positions, grad_out):
        seqs, blk, heads, head = query.shape
        rows = blk * heads
        chips = cp // CORES
        mine = seqs // CORES
        keys = cp * blk
        freq = np.power(float(ROPE_BASE), -2.0 * np.arange(head // 2) / head)
        freq = jnp.asarray(np.concatenate([freq, freq])[None, :].astype(np.float32))
        vmem = pl.BlockSpec(memory_space=pltpu.VMEM)
        hbm = pl.BlockSpec(memory_space=pltpu.HBM)
        dma = pltpu.SemaphoreType.DMA
        big = jax.ShapeDtypeStruct((seqs, rows, head), BF16)
        small = jax.ShapeDtypeStruct((seqs, blk, head), BF16)
        o_mid, dq_mid, rbuf, tabs = pl.pallas_call(
            functools.partial(attend_kernel, cp, blk),
            out_shape=[big, big, jax.ShapeDtypeStruct((chips, seqs, 2, blk, head), F32),
                       jax.ShapeDtypeStruct((2, blk, head), F32)],
            in_specs=[hbm] * 6,
            out_specs=[vmem, vmem, vmem, vmem],
            scratch_shapes=[
                pltpu.VMEM((seqs, blk, head), BF16),
                pltpu.VMEM((seqs, blk, head), BF16),
                pltpu.VMEM((1, blk), jnp.int32),
                pltpu.VMEM((1, head), F32),
                pltpu.VMEM((mine, CORES, rows, head), BF16),
                pltpu.VMEM((mine, CORES, rows, head), BF16),
                pltpu.VMEM((mine, CORES * rows, head), BF16),
                pltpu.VMEM((CORES, 2, blk, head), F32),
                pltpu.VMEM((seqs, 2, blk, head), BF16),
                pltpu.VMEM((mine, cp, 2, blk, head), BF16),
                pltpu.VMEM((mine, keys, CORES * rows), BF16),
                pltpu.VMEM((mine, keys, CORES * rows), BF16),
                pltpu.VMEM((mine, cp, 2, blk, head), F32),
                pltpu.VMEM((mine, rows, head), BF16),
                pltpu.VMEM((mine, rows, head), BF16),
                dma((4,)), dma((2, mine)), dma((2, mine)), dma((2, mine)), dma, dma,
                dma((mine, chips, CORES)), dma((mine, cp)),
                dma((mine, 2, chips, CORES)), dma((chips, seqs, 2)),
                dma((2, mine)), dma((2, mine)),
            ],
            compiler_params=pltpu.CompilerParams(collective_id=0, has_side_effects=True,
                                                 vmem_limit_bytes=32 * 2 ** 20),
            name="attend",
        )(*(pltpu.with_memory_space_constraint(a, pltpu.HBM) for a in (
            query.reshape(seqs, rows, head), grad_out.reshape(seqs, rows, head), key, value,
            positions.reshape(1, blk), freq)))
        attn, dquery, dkey, dvalue = pl.pallas_call(
            finish_kernel,
            out_shape=[big, big, small, small],
            in_specs=[vmem] * 4,
            out_specs=[hbm, hbm, vmem, vmem],
            scratch_shapes=[dma((2,))],
            compiler_params=pltpu.CompilerParams(vmem_limit_bytes=16 * 2 ** 20),
            name="finish",
        )(o_mid, dq_mid, rbuf, tabs)
        shape = (seqs, blk, heads, head)
        return attn.reshape(shape), dquery.reshape(shape), dkey, dvalue

    return jax.shard_map(per_device, mesh=mesh, in_specs=(query_spec, kv_spec, kv_spec, pos_spec, query_spec),
                         out_specs=(query_spec, query_spec, kv_spec, kv_spec), check_vma=False)
```

time: 159 us -> 23.6 us (0.15); the launches traced: 156 us -> 23.5 us
  starting transfers between devices: 94.4 us -> 0 us
  Pallas kernels: 0 us -> 22.9 us
  matrix products: 17.3 us -> 0 us
  waiting for transfers between devices: 16.5 us -> 0 us
  local copies, waits for them, and re-layouts: 14.3 us -> 0 us
  other arithmetic: 12.1 us -> 0 us
    ppermute x44 -> x0, starting transfers between devices: 94.4 us -> none  [the longest x28 55.9 us: backward_step(): lax.ppermute((key_blk, value_blk, dkey_blk, dvalue_blk), 'cp', shift_pairs)]
    pallas_call x0 -> x2, Pallas kernels: none -> 22.9 us  [the longest x1 20.9 us: per_device(): pl.pallas_call(functools.partial(attend_kernel, cp, blk), out_shape=[big,...]
    dot_general x13 -> x0, matrix products: 17.3 us -> none  [the longest x2 4.86 us: backward_block(): jnp.einsum('cril,crie->cle', probs_f.astype(jnp.bfloat16), grad_out, pref...]
    ppermute x44 -> x0, waiting for transfers between devices: 16.5 us -> none  [the longest x28 8.61 us: backward_step(): lax.ppermute((key_blk, value_blk, dkey_blk, dvalue_blk), 'cp', shift_pairs)]
    while x44 -> x0, local copies, waits for them, and re-layouts: 11.6 us -> none
    convert_element_type x5 -> x0, other arithmetic: 4.01 us -> none  [the longest x1 1.7 us: per_device(): grad_query = rotate(bwd_carry[2], cos_q, -sin_q).astype(jnp.bfloat16)]
    neg x5 -> x0, other arithmetic: 3.76 us -> none  [the longest x4 3 us: rotate(): -values[..., half_dim:]]
    unnamed x23 -> x0, local copies, waits for them, and re-layouts: 2.04 us -> none
  transfers between devices with their start and end apart: 44 -> 0, of which waited for: 25 -> 0; matrix products, arithmetic and copies ran while one was open for 2% -> 0% of each run, Pallas kernels for 0% -> 0%
where the time goes in v1:
time: 23.6 us; the launch traced here: 23.5 us
  Pallas kernels  22.9 us (97%)
  between operations  0.64 us (3%)
    pallas_call x1, Pallas kernels, per_device(): pl.pallas_call(functools.partial(attend_kernel, cp, blk), out_shape=[big,...  20.9 us
    pallas_call x1, Pallas kernels, per_device(): pl.pallas_call(finish_kernel, out_shape=[big, big, small, small], in_spec...  1.97 us

profile of v1, /device:TPU:113, one launch (start us, length us, event | category | flops | bytes accessed | tf_op | source)
XLA Modules:
  0.0 23.5 jit_solution(7727329963811904931)
XLA Ops:
  0.6 20.9 %attend.1 = (bf16[4,1024,128]{2,1,0:T(8,128)(2,1)S(1)}, bf16[4,1024,128]{2,1,0:T(8,128)(2,1)S(1)}, f32[4,4,2,32,128]{4,3,2,1,0:T(8,128)S(1)}, f32[2,32,128]{2,1,0:T(8,128)S(1)}) custom-call(bf16[4,1024,128]{2,1,0:T(8,128)(2,1)} %bitcast.5, bf16[4,1024,128]{2,1,0:T(8,128)(2,1)} %bitcast.6, bf16[4,32,128]{2,1,0:T(8,128)(2,1)} %k_hbm.1, ...), custom_call_target="tpu_custom_call" | custom-call | tf_op jit(solution)/shard_map/attend/pallas_call | solution.py:278
  21.5 2.0 %finish.1 = (bf16[4,1024,128]{2,1,0:T(8,128)(2,1)}, bf16[4,1024,128]{2,1,0:T(8,128)(2,1)}, bf16[4,32,128]{2,1,0:T(8,128)(2,1)}, bf16[4,32,128]{2,1,0:T(8,128)(2,1)}) custom-call(bf16[4,1024,128]{2,1,0:T(8,128)(2,1)S(1)} %get-tuple-element.12.o_in, bf16[4,1024,128]{2,1,0:T(8,128)(2,1)S(1)} %get-tuple-element.13.dq_in, ...), custom_call_target="tpu_custom_call" | custom-call | tf_op jit(solution)/shard_map/finish/pallas_call | solution.py:311

commit v2 on v1

v2 whole, which is shorter than its diff:
```python
import functools

import jax
import jax.numpy as jnp
import numpy as np
from jax import lax
from jax.experimental import pallas as pl
from jax.experimental.pallas import tpu as pltpu
from jax.sharding import PartitionSpec as P

ROPE_BASE = 10000
CORES = 2
LOG2E = 1.4426950408889634
F32 = jnp.float32
BF16 = jnp.bfloat16
ROWS = 1024


def dot_nn(a, b):
    return jnp.dot(a, b, preferred_element_type=F32)


def dot_nt(a, b):
    return lax.dot_general(a, b, (((1,), (1,)), ((), ())), preferred_element_type=F32)


def attend_kernel(cp, blk, q_hbm, g_hbm, k_hbm, v_hbm, pos_hbm, freq_hbm,
                  o_ref, dq_ref, rbuf, tabs_out,
                  kv_in, pos_ref, freq_ref, qg, rq, tabs, kvown, kvb, g_t, tab_t, diff,
                  w_t, p_f, norm, p_t, ds_t, o_t, part, osib, dqsib,
                  first_sem, loc_sem, qg_send, qg_recv, tab_sem, kv_send, kv_recv,
                  r_sem, od_sem):
    chips = cp // CORES
    seqs = q_hbm.shape[0]
    mine = seqs // CORES
    rows, head = q_hbm.shape[1], q_hbm.shape[2]
    heads = rows // blk
    half_dim = head // 2
    keys = cp * blk
    scale = head ** -0.5
    me = lax.axis_index("cp")
    chip = lax.div(me, CORES)
    core = lax.rem(me, CORES)
    sib = chip * CORES + 1 - core

    barrier = pltpu.get_barrier_semaphore()
    for d in range(1, cp):
        pl.semaphore_signal(barrier, inc=1, device_id={"cp": lax.rem(me + d, cp)},
                            device_id_type=pl.DeviceIdType.MESH)

    def remote(src, dst, ssem, rsem, dev):
        return pltpu.make_async_remote_copy(src_ref=src, dst_ref=dst, send_sem=ssem, recv_sem=rsem,
                                            device_id={"cp": dev}, device_id_type=pl.DeviceIdType.MESH)

    def wait_bytes(ref, sem):
        pltpu.make_async_copy(ref, ref, sem).wait()

    def wait_by_chip(ref, sem, blocks):
        for c in range(chips):
            @pl.when(chip == c)
            def _():
                wait_bytes(ref.at[pl.ds(0, blocks(c))], sem)

    first = [pltpu.make_async_copy(pos_hbm, pos_ref, first_sem.at[0]),
             pltpu.make_async_copy(freq_hbm, freq_ref, first_sem.at[1]),
             pltpu.make_async_copy(k_hbm, kv_in.at[0], first_sem.at[2]),
             pltpu.make_async_copy(v_hbm, kv_in.at[1], first_sem.at[2])]
    for c in first:
        c.start()
    for n, src in enumerate((q_hbm, g_hbm)):
        for s in range(mine):
            pltpu.make_async_copy(src.at[core * mine + s], qg.at[n, s, 0], loc_sem).start()

    for d in range(1, chips):
        @pl.when(d > chip)
        def _():
            for n in range(2 * mine):
                kvb[n * cp + d * CORES:n * cp + (d + 1) * CORES] = jnp.zeros((CORES, blk, head), BF16)

        @pl.when(chip + d >= chips)
        def _():
            rbuf[d * seqs * 2:(d + 1) * seqs * 2] = jnp.zeros((seqs * 2, blk, head), F32)

    first[0].wait()
    first[1].wait()
    pos_row = jnp.broadcast_to(pos_ref[...].astype(F32), (blk, blk))
    ident = lax.broadcasted_iota(jnp.int32, (blk, blk), 0) == lax.broadcasted_iota(jnp.int32, (blk, blk), 1)
    pos_col = jnp.sum(jnp.where(ident, pos_row, 0.0), axis=1, keepdims=True)
    ang = pos_col * freq_ref[...]
    cos_t = jnp.cos(ang)
    lane = lax.broadcasted_iota(jnp.int32, (blk, head), 1)
    sin_t = jnp.where(lane < half_dim, -jnp.sin(ang), jnp.sin(ang))
    tabs[0, 0] = cos_t
    tabs[0, 1] = sin_t
    tabs_out[0] = cos_t
    tabs_out[1] = sin_t
    wait_bytes(kv_in, first_sem.at[2])
    for b in range(seqs):
        kf = kv_in[0, b].astype(F32)
        kvown[b, 0] = (kf * cos_t + pltpu.roll(kf, half_dim, 1) * sin_t).astype(BF16)
        kvown[b, 1] = kv_in[1, b]

    pl.semaphore_wait(barrier, cp - 1)

    def kv_wave(s, n):
        base = (s * 2 + n) * cp
        for d in range(chips - 1, 0, -1):
            @pl.when(chip + d < chips)
            def _():
                for k2 in range(CORES):
                    remote(kvown.at[k2 * mine + s, n], kvb.at[base + d * CORES + core], kv_send, kv_recv.at[s, n],
                           (chip + d) * CORES + k2).start()
        remote(kvown.at[(1 - core) * mine + s, n], kvb.at[base + core], kv_send, kv_recv.at[s, n], sib).start()

    def kv_wait(s, n):
        wait_by_chip(kvb, kv_recv.at[s, n], lambda c: CORES * c + 1)

    tab_copy = remote(tabs.at[0], tabs.at[1], tab_sem.at[0], tab_sem.at[1], sib)

    kv_wave(0, 0)
    tab_copy.start()
    for s in range(mine):
        for n, src in enumerate((q_hbm, g_hbm)):
            remote(src.at[(1 - core) * mine + s], qg.at[n, s, 1], qg_send, qg_recv.at[s], sib).start()
    for s in range(mine):
        for n in range(2):
            kvb[(s * 2 + n) * cp + core] = kvown[core * mine + s, n]

    def wide(tab):
        return jnp.broadcast_to(tab[:, None, :], (blk, heads, head)).reshape(rows, head)

    def prepare(s, h, cos_q, sin_q):
        x = qg[0, s, h].astype(F32)
        rq[s, h * rows:(h + 1) * rows, :] = (x * cos_q + pltpu.roll(x, half_dim, 1) * sin_q).astype(BF16)
        g_t[s, :, h * rows:(h + 1) * rows] = qg[1, s, h].T

    def tables(h):
        cos_b, sin_b = tabs[h, 0], tabs[h, 1]
        tab_t[:, h * rows:(h + 1) * rows] = wide(jnp.where(lane < half_dim, cos_b, sin_b) * scale).T
        return wide(cos_b), wide(sin_b)

    diff[...] = lax.broadcasted_iota(jnp.int32, (blk, rows), 0) - lax.div(
        lax.broadcasted_iota(jnp.int32, (blk, rows), 1), heads)
    wait_bytes(qg.at[0], loc_sem)
    cs = tables(0)
    prepare(0, 0, *cs)
    kv_wave(0, 1)
    for s in range(1, mine):
        prepare(s, 0, *cs)
    tab_copy.wait_recv()
    cs = tables(1)
    for s in range(mine):
        wait_bytes(qg.at[0, 0], qg_recv.at[s])
        prepare(s, 1, *cs)
        if s + 1 < mine:
            kv_wave(s + 1, 0)
    for s in range(1, mine):
        kv_wave(s, 1)

    def send_part(s, x):
        base = (s * 2 + x) * cp
        slot = (core * mine + s) * 2 + x
        for d in range(chips - 1, 0, -1):
            @pl.when(chip >= d)
            def _():
                for k2 in range(CORES):
                    remote(part.at[base + d * CORES + k2], rbuf.at[d * seqs * 2 + slot], r_sem.at[0], r_sem.at[1],
                           (chip - d) * CORES + k2).start()
        remote(part.at[base + 1 - core], rbuf.at[slot], r_sem.at[0], r_sem.at[1], sib).start()
        rbuf[slot] = part[base + core]

    def out_copy(src, dst, s):
        return remote(src.at[s], dst.at[core * mine + s], od_sem.at[0], od_sem.at[1], sib)

    for s in range(mine):
        kv_wait(s, 0)
        kk = kvb[s * 2 * cp:(s * 2 + 1) * cp].reshape(keys, head)
        for h in (1, 0):
            owner = core if h == 0 else 1 - core
            for r in range(0, rows, ROWS):
                row0 = h * rows + r
                x = dot_nt(kk, rq[s, row0:row0 + ROWS, :])
                dif = diff[:, r:r + ROWS]
                pieces = [jnp.where(dif <= (owner - k) * blk, x[k * blk:(k + 1) * blk], -jnp.inf)
                          for k in range(CORES)]
                for d in range(1, chips):
                    bias = jnp.where(d <= chip, 0.0, -jnp.inf)
                    pieces.append(x[d * CORES * blk:(d + 1) * CORES * blk] + bias)
                x = jnp.concatenate(pieces, axis=0)
                mx = jnp.max(x, axis=0, keepdims=True)
                w = jnp.exp2((x - mx) * (scale * LOG2E))
                inv_l = 1.0 / jnp.sum(w, axis=0, keepdims=True)
                w_t[:, row0:row0 + ROWS] = w.astype(BF16)
                p = w * inv_l
                p_f[:, row0:row0 + ROWS] = p
                p_t[:, row0:row0 + ROWS] = p.astype(BF16)
                norm[:, row0:row0 + ROWS] = inv_l
        part[(s * 2 + 1) * cp:(s * 2 + 2) * cp] = dot_nn(
            p_t[...], qg[1, s].reshape(CORES * rows, head)).reshape(cp, blk, head)
        send_part(s, 1)
        kv_wait(s, 1)
        vv = kvb[(s * 2 + 1) * cp:(s * 2 + 2) * cp].reshape(keys, head)
        v_t = vv.T
        for h in (1, 0):
            for r in range(0, rows, ROWS):
                row0 = h * rows + r
                ot = (dot_nn(v_t, w_t[:, row0:row0 + ROWS]) * norm[:, row0:row0 + ROWS]).astype(BF16)
                o_t[s, :, row0:row0 + ROWS] = ot
                delta = jnp.sum(g_t[s, :, row0:row0 + ROWS].astype(F32) * ot.astype(F32), axis=0, keepdims=True)
                dp = dot_nt(vv, qg[1, s, h, r:r + ROWS, :])
                ds_t[s, :, row0:row0 + ROWS] = (p_f[:, row0:row0 + ROWS] * (dp - delta)).astype(BF16)
        part[s * 2 * cp:(s * 2 + 1) * cp] = dot_nn(ds_t[s], rq[s]).reshape(cp, blk, head)
        send_part(s, 0)

    for s in range(mine):
        k_t = kvb[s * 2 * cp:(s * 2 + 1) * cp].reshape(keys, head).T
        for h in (1, 0):
            for r in range(0, rows, ROWS):
                row0 = h * rows + r
                dq_t = dot_nn(k_t, ds_t[s, :, row0:row0 + ROWS])
                cos_q = tab_t[:half_dim, row0:row0 + ROWS]
                sin_q = tab_t[half_dim:, row0:row0 + ROWS]
                top, low = dq_t[:half_dim], dq_t[half_dim:]
                dq = jnp.concatenate([top * cos_q + low * sin_q, low * cos_q - top * sin_q], axis=0).astype(BF16).T
                out = o_t[s, :, row0:row0 + ROWS].T
                if h == 0:
                    dq_ref[core * mine + s, r:r + ROWS, :] = dq
                    o_ref[core * mine + s, r:r + ROWS, :] = out
                else:
                    dqsib[s, r:r + ROWS, :] = dq
                    osib[s, r:r + ROWS, :] = out
            if h == 1:
                out_copy(osib, o_ref, s).start()
                out_copy(dqsib, dq_ref, s).start()

    tab_copy.wait_send()
    wait_bytes(qg.at[0], qg_send)
    wait_by_chip(kvb, kv_send, lambda c: 2 * mine * (CORES * (chips - 1 - c) + 1))
    wait_bytes(qg.at[0], od_sem.at[0])
    wait_bytes(qg.at[0], od_sem.at[1])
    wait_by_chip(part, r_sem.at[0], lambda c: 2 * mine * (CORES * c + 1))
    wait_by_chip(rbuf, r_sem.at[1], lambda c: 2 * mine * (CORES * (chips - 1 - c) + 1))


def finish_kernel(o_in, dq_in, rbuf, tabs, o_hbm, dq_hbm, dk_hbm, dv_hbm, dk_buf, dv_buf, sem):
    copies = [pltpu.make_async_copy(o_in, o_hbm, sem.at[0]), pltpu.make_async_copy(dq_in, dq_hbm, sem.at[1]),
              pltpu.make_async_copy(dk_buf, dk_hbm, sem.at[2]), pltpu.make_async_copy(dv_buf, dv_hbm, sem.at[3])]
    for c in copies[:2]:
        c.start()
    head = tabs.shape[-1]
    scale = head ** -0.5
    cos_t, sin_t = tabs[0], tabs[1]
    seqs = dk_buf.shape[0]
    for b in range(seqs):
        dk = rbuf[2 * b]
        dv = rbuf[2 * b + 1]
        for c in range(2 * seqs, rbuf.shape[0], 2 * seqs):
            dk = dk + rbuf[c + 2 * b]
            dv = dv + rbuf[c + 2 * b + 1]
        dk = dk * scale
        dk_buf[b] = (dk * cos_t - pltpu.roll(dk, head // 2, 1) * sin_t).astype(BF16)
        dv_buf[b] = dv.astype(BF16)
    for c in copies[2:]:
        c.start()
    for c in copies:
        c.wait()


def solution(mesh):
    cp = mesh.shape["cp"]
    query_spec = P("dp", "cp", None, None)
    kv_spec = P("dp", "cp", None)
    pos_spec = P(("dp", "cp"))

    def per_device(query, key, value, positions, grad_out):
        seqs, blk, heads, head = query.shape
        rows = blk * heads
        chips = cp // CORES
        mine = seqs // CORES
        keys = cp * blk
        freq = np.power(float(ROPE_BASE), -2.0 * np.arange(head // 2) / head)
        freq = jnp.asarray(np.concatenate([freq, freq])[None, :].astype(np.float32))
        vmem = pl.BlockSpec(memory_space=pltpu.VMEM)
        hbm = pl.BlockSpec(memory_space=pltpu.HBM)
        dma = pltpu.SemaphoreType.DMA
        big = jax.ShapeDtypeStruct((seqs, rows, head), BF16)
        small = jax.ShapeDtypeStruct((seqs, blk, head), BF16)
        o_mid, dq_mid, rbuf, tabs = pl.pallas_call(
            functools.partial(attend_kernel, cp, blk),
            out_shape=[big, big, jax.ShapeDtypeStruct((chips * seqs * 2, blk, head), F32),
                       jax.ShapeDtypeStruct((2, blk, head), F32)],
            in_specs=[hbm] * 6,
            out_specs=[vmem, vmem, vmem, vmem],
            scratch_shapes=[
                pltpu.VMEM((2, seqs, blk, head), BF16),
                pltpu.VMEM((1, blk), jnp.int32),
                pltpu.VMEM((1, head), F32),
                pltpu.VMEM((2, mine, CORES, rows, head), BF16),
                pltpu.VMEM((mine, CORES * rows, head), BF16),
                pltpu.VMEM((CORES, 2, blk, head), F32),
                pltpu.VMEM((seqs, 2, blk, head), BF16),
                pltpu.VMEM((mine * 2 * cp, blk, head), BF16),
                pltpu.VMEM((mine, head, CORES * rows), BF16),
                pltpu.VMEM((head, CORES * rows), F32),
                pltpu.VMEM((blk, rows), jnp.int32),
                pltpu.VMEM((keys, CORES * rows), BF16),
                pltpu.VMEM((keys, CORES * rows), F32),
                pltpu.VMEM((1, CORES * rows), F32),
                pltpu.VMEM((keys, CORES * rows), BF16),
                pltpu.VMEM((mine, keys, CORES * rows), BF16),
                pltpu.VMEM((mine, head, CORES * rows), BF16),
                pltpu.VMEM((mine * 2 * cp, blk, head), F32),
                pltpu.VMEM((mine, rows, head), BF16),
                pltpu.VMEM((mine, rows, head), BF16),
                dma((3,)), dma, dma, dma((mine,)), dma((2,)), dma, dma((mine, 2)), dma((2,)), dma((2,)),
            ],
            compiler_params=pltpu.CompilerParams(collective_id=0, has_side_effects=True,
                                                 vmem_limit_bytes=32 * 2 ** 20),
            name="attend",
        )(*(pltpu.with_memory_space_constraint(a, pltpu.HBM) for a in (
            query.reshape(seqs, rows, head), grad_out.reshape(seqs, rows, head), key, value,
            positions.reshape(1, blk), freq)))
        attn, dquery, dkey, dvalue = pl.pallas_call(
            finish_kernel,
            out_shape=[big, big, small, small],
            in_specs=[vmem] * 4,
            out_specs=[hbm] * 4,
            scratch_shapes=[pltpu.VMEM((seqs, blk, head), BF16), pltpu.VMEM((seqs, blk, head), BF16), dma((4,))],
            compiler_params=pltpu.CompilerParams(vmem_limit_bytes=16 * 2 ** 20),
            name="finish",
        )(o_mid, dq_mid, rbuf, tabs)
        shape = (seqs, blk, heads, head)
        return attn.reshape(shape), dquery.reshape(shape), dkey, dvalue

    return jax.shard_map(per_device, mesh=mesh, in_specs=(query_spec, kv_spec, kv_spec, pos_spec, query_spec),
                         out_specs=(query_spec, query_spec, kv_spec, kv_spec), check_vma=False)
```

time: 23.6 us -> 20 us (0.85)
  Pallas kernels: 22.9 us -> 19.2 us
    pallas_call x1, Pallas kernels: 20.9 us -> 17.9 us  [per_device(): pl.pallas_call(functools.partial(attend_kernel, cp, blk), out_shape=[big,...]
    pallas_call x1, Pallas kernels: 1.97 us -> 1.36 us  [per_device(): pl.pallas_call(finish_kernel, out_shape=[big, big, small, small], in_spec...]
where the time goes in v2:
time: 20 us; the launch traced here: 19.9 us
  Pallas kernels  19.2 us (96%)
  between operations  0.64 us (3%)
    pallas_call x1, Pallas kernels, per_device(): pl.pallas_call(functools.partial(attend_kernel, cp, blk), out_shape=[big,...  17.9 us
    pallas_call x1, Pallas kernels, per_device(): pl.pallas_call(finish_kernel, out_shape=[big, big, small, small], in_spec...  1.36 us

profile of v2, /device:TPU:113, one launch (start us, length us, event | category | flops | bytes accessed | tf_op | source)
XLA Modules:
  0.0 19.9 jit_solution(11088517516919259282)
XLA Ops:
  0.6 17.9 %attend.1 = (bf16[4,1024,128]{2,1,0:T(8,128)(2,1)S(1)}, bf16[4,1024,128]{2,1,0:T(8,128)(2,1)S(1)}, f32[32,32,128]{2,1,0:T(8,128)S(1)}, f32[2,32,128]{2,1,0:T(8,128)S(1)}) custom-call(bf16[4,1024,128]{2,1,0:T(8,128)(2,1)} %bitcast.5, bf16[4,1024,128]{2,1,0:T(8,128)(2,1)} %bitcast.6, bf16[4,32,128]{2,1,0:T(8,128)(2,1)} %k_hbm.1, bf16[4,32,128]{2,1,0:T(8,128)(2,1)} %v_hbm.1, ...), custom_call_target="tpu_custom_call" | custom-call | tf_op jit(solution)/shard_map/attend/pallas_call | solution.py:288
  18.5 1.4 %finish.1 = (bf16[4,1024,128]{2,1,0:T(8,128)(2,1)}, bf16[4,1024,128]{2,1,0:T(8,128)(2,1)}, bf16[4,32,128]{2,1,0:T(8,128)(2,1)}, bf16[4,32,128]{2,1,0:T(8,128)(2,1)}) custom-call(bf16[4,1024,128]{2,1,0:T(8,128)(2,1)S(1)} %get-tuple-element.12.o_in, bf16[4,1024,128]{2,1,0:T(8,128)(2,1)S(1)} %get-tuple-element.13.dq_in, ...), custom_call_target="tpu_custom_call" | custom-call | tf_op jit(solution)/shard_map/finish/pallas_call | solution.py:323

commit v3 on v2

--- a/solution.py
+++ b/solution.py
@@ -13,7 +13,9 @@
 LOG2E = 1.4426950408889634
 F32 = jnp.float32
 BF16 = jnp.bfloat16
-ROWS = 1024
+ROWS = 512
+LANES = 128
+RELAYED = (1,)
 
 
 def dot_nn(a, b):
@@ -22,14 +24,23 @@
 
 def dot_nt(a, b):
     return lax.dot_general(a, b, (((1,), (1,)), ((), ())), preferred_element_type=F32)
+
+
+def put(ref, row0, val):
+    for n in range(0, val.shape[1], LANES):
+        ref[(row0 + n) // LANES] = val[:, n:n + LANES]
+
+
+def get(ref, row0, count):
+    return jnp.concatenate([ref[(row0 + n) // LANES] for n in range(0, count, LANES)], axis=1)
 
 
 def attend_kernel(cp, blk, q_hbm, g_hbm, k_hbm, v_hbm, pos_hbm, freq_hbm,
                   o_ref, dq_ref, rbuf, tabs_out,
                   kv_in, pos_ref, freq_ref, qg, rq, tabs, kvown, kvb, g_t, tab_t, diff,
-                  w_t, p_f, norm, p_t, ds_t, o_t, part, osib, dqsib,
+                  w_t, p_f, norm, p_t, ds_t, o_t, part, passing, osib, dqsib,
                   first_sem, loc_sem, qg_send, qg_recv, tab_sem, kv_send, kv_recv,
-                  r_sem, od_sem):
+                  r_sem, pass_sem, od_sem):
     chips = cp // CORES
     seqs = q_hbm.shape[0]
     mine = seqs // CORES
@@ -76,6 +87,13 @@
         def _():
             for n in range(2 * mine):
                 kvb[n * cp + d * CORES:n * cp + (d + 1) * CORES] = jnp.zeros((CORES, blk, head), BF16)
+
+        if d == chips - 2:
+            @pl.when(chip == 0)
+            def _():
+                for k2 in range(CORES):
+                    for x in RELAYED:
+                        rbuf[(d * seqs + k2 * mine) * 2 + x] = jnp.zeros((blk, head), F32)
 
         @pl.when(chip + d >= chips)
         def _():
@@ -132,15 +150,15 @@
     def prepare(s, h, cos_q, sin_q):
         x = qg[0, s, h].astype(F32)
         rq[s, h * rows:(h + 1) * rows, :] = (x * cos_q + pltpu.roll(x, half_dim, 1) * sin_q).astype(BF16)
-        g_t[s, :, h * rows:(h + 1) * rows] = qg[1, s, h].T
+        put(g_t.at[s], h * rows, qg[1, s, h].T)
 
     def tables(h):
         cos_b, sin_b = tabs[h, 0], tabs[h, 1]
-        tab_t[:, h * rows:(h + 1) * rows] = wide(jnp.where(lane < half_dim, cos_b, sin_b) * scale).T
+        put(tab_t, h * rows, wide(jnp.where(lane < half_dim, cos_b, sin_b) * scale).T)
         return wide(cos_b), wide(sin_b)
 
-    diff[...] = lax.broadcasted_iota(jnp.int32, (blk, rows), 0) - lax.div(
-        lax.broadcasted_iota(jnp.int32, (blk, rows), 1), heads)
+    put(diff, 0, lax.broadcasted_iota(jnp.int32, (blk, rows), 0) - lax.div(
+        lax.broadcasted_iota(jnp.int32, (blk, rows), 1), heads))
     wait_bytes(qg.at[0], loc_sem)
     cs = tables(0)
     prepare(0, 0, *cs)
@@ -157,15 +175,37 @@
     for s in range(1, mine):
         kv_wave(s, 1)
 
+    origin = chips - 2
+    middle = origin - 1
+
+    def send_far(s, x, d):
+        base = (s * 2 + x) * cp
+        slot = (core * mine + s) * 2 + x
+        for k2 in range(CORES):
+            remote(part.at[base + d * CORES + k2], rbuf.at[d * seqs * 2 + slot], r_sem.at[0], r_sem.at[1],
+                   (chip - d) * CORES + k2).start()
+
     def send_part(s, x):
         base = (s * 2 + x) * cp
         slot = (core * mine + s) * 2 + x
+        relayed = s == 0 and x in RELAYED
         for d in range(chips - 1, 0, -1):
-            @pl.when(chip >= d)
+            direct = chip >= d
+            if relayed and d == origin:
+                direct = jnp.logical_and(direct, chip != origin)
+
+                @pl.when(chip == origin)
+                def _():
+                    n = RELAYED.index(x) * CORES
+                    for k2 in range(CORES):
+                        remote(part.at[base + d * CORES + k2], passing.at[n + k2], r_sem.at[0], pass_sem,
+                               middle * CORES + core).start()
+            if relayed and d == middle:
+                direct = jnp.logical_and(direct, chip != middle)
+
+            @pl.when(direct)
             def _():
-                for k2 in range(CORES):
-                    remote(part.at[base + d * CORES + k2], rbuf.at[d * seqs * 2 + slot], r_sem.at[0], r_sem.at[1],
-                           (chip - d) * CORES + k2).start()
+                send_far(s, x, d)
         remote(part.at[base + 1 - core], rbuf.at[slot], r_sem.at[0], r_sem.at[1], sib).start()
         rbuf[slot] = part[base + core]
 
@@ -175,12 +215,12 @@
     for s in range(mine):
         kv_wait(s, 0)
         kk = kvb[s * 2 * cp:(s * 2 + 1) * cp].reshape(keys, head)
-        for h in (1, 0):
+        for h in (0, 1):
             owner = core if h == 0 else 1 - core
             for r in range(0, rows, ROWS):
                 row0 = h * rows + r
                 x = dot_nt(kk, rq[s, row0:row0 + ROWS, :])
-                dif = diff[:, r:r + ROWS]
+                dif = get(diff, r, ROWS)
                 pieces = [jnp.where(dif <= (owner - k) * blk, x[k * blk:(k + 1) * blk], -jnp.inf)
                           for k in range(CORES)]
                 for d in range(1, chips):
@@ -190,39 +230,47 @@
                 mx = jnp.max(x, axis=0, keepdims=True)
                 w = jnp.exp2((x - mx) * (scale * LOG2E))
                 inv_l = 1.0 / jnp.sum(w, axis=0, keepdims=True)
-                w_t[:, row0:row0 + ROWS] = w.astype(BF16)
+                put(w_t, row0, w.astype(BF16))
                 p = w * inv_l
-                p_f[:, row0:row0 + ROWS] = p
-                p_t[:, row0:row0 + ROWS] = p.astype(BF16)
+                put(p_f, row0, p)
+                put(p_t, row0, p.astype(BF16))
                 norm[:, row0:row0 + ROWS] = inv_l
         part[(s * 2 + 1) * cp:(s * 2 + 2) * cp] = dot_nn(
-            p_t[...], qg[1, s].reshape(CORES * rows, head)).reshape(cp, blk, head)
+            get(p_t, 0, CORES * rows), qg[1, s].reshape(CORES * rows, head)).reshape(cp, blk, head)
         send_part(s, 1)
         kv_wait(s, 1)
         vv = kvb[(s * 2 + 1) * cp:(s * 2 + 2) * cp].reshape(keys, head)
         v_t = vv.T
-        for h in (1, 0):
+        for h in (0, 1):
             for r in range(0, rows, ROWS):
                 row0 = h * rows + r
-                ot = (dot_nn(v_t, w_t[:, row0:row0 + ROWS]) * norm[:, row0:row0 + ROWS]).astype(BF16)
-                o_t[s, :, row0:row0 + ROWS] = ot
-                delta = jnp.sum(g_t[s, :, row0:row0 + ROWS].astype(F32) * ot.astype(F32), axis=0, keepdims=True)
+                ot = (dot_nn(v_t, get(w_t, row0, ROWS)) * norm[:, row0:row0 + ROWS]).astype(BF16)
+                put(o_t.at[s], row0, ot)
+                delta = jnp.sum(get(g_t.at[s], row0, ROWS).astype(F32) * ot.astype(F32), axis=0, keepdims=True)
                 dp = dot_nt(vv, qg[1, s, h, r:r + ROWS, :])
-                ds_t[s, :, row0:row0 + ROWS] = (p_f[:, row0:row0 + ROWS] * (dp - delta)).astype(BF16)
-        part[s * 2 * cp:(s * 2 + 1) * cp] = dot_nn(ds_t[s], rq[s]).reshape(cp, blk, head)
+                put(ds_t.at[s], row0, (get(p_f, row0, ROWS) * (dp - delta)).astype(BF16))
+        part[s * 2 * cp:(s * 2 + 1) * cp] = dot_nn(get(ds_t.at[s], 0, CORES * rows), rq[s]).reshape(cp, blk, head)
         send_part(s, 0)
+
+    @pl.when(chip == middle)
+    def _():
+        wait_bytes(passing, pass_sem)
+        for n, x in enumerate(RELAYED):
+            first_slot = x * cp + middle * CORES
+            part[first_slot:first_slot + CORES] += passing[n * CORES:(n + 1) * CORES]
+            send_far(0, x, middle)
 
     for s in range(mine):
         k_t = kvb[s * 2 * cp:(s * 2 + 1) * cp].reshape(keys, head).T
         for h in (1, 0):
             for r in range(0, rows, ROWS):
                 row0 = h * rows + r
-                dq_t = dot_nn(k_t, ds_t[s, :, row0:row0 + ROWS])
-                cos_q = tab_t[:half_dim, row0:row0 + ROWS]
-                sin_q = tab_t[half_dim:, row0:row0 + ROWS]
+                dq_t = dot_nn(k_t, get(ds_t.at[s], row0, ROWS))
+                tab = get(tab_t, row0, ROWS)
+                cos_q, sin_q = tab[:half_dim], tab[half_dim:]
                 top, low = dq_t[:half_dim], dq_t[half_dim:]
                 dq = jnp.concatenate([top * cos_q + low * sin_q, low * cos_q - top * sin_q], axis=0).astype(BF16).T
-                out = o_t[s, :, row0:row0 + ROWS].T
+                out = get(o_t.at[s], row0, ROWS).T
                 if h == 0:
                     dq_ref[core * mine + s, r:r + ROWS, :] = dq
                     o_ref[core * mine + s, r:r + ROWS, :] = out
@@ -239,7 +287,8 @@
     wait_bytes(qg.at[0], od_sem.at[0])
     wait_bytes(qg.at[0], od_sem.at[1])
     wait_by_chip(part, r_sem.at[0], lambda c: 2 * mine * (CORES * c + 1))
-    wait_by_chip(rbuf, r_sem.at[1], lambda c: 2 * mine * (CORES * (chips - 1 - c) + 1))
+    wait_by_chip(rbuf, r_sem.at[1], lambda c: 2 * mine * (CORES * (chips - 1 - c) + 1)
+                 - (CORES * len(RELAYED) if c == 0 else 0))
 
 
 def finish_kernel(o_in, dq_in, rbuf, tabs, o_hbm, dq_hbm, dk_hbm, dv_hbm, dk_buf, dv_buf, sem):
@@ -278,6 +327,7 @@
         chips = cp // CORES
         mine = seqs // CORES
         keys = cp * blk
+        tiles = CORES * rows // LANES
         freq = np.power(float(ROPE_BASE), -2.0 * np.arange(head // 2) / head)
         freq = jnp.asarray(np.concatenate([freq, freq])[None, :].astype(np.float32))
         vmem = pl.BlockSpec(memory_space=pltpu.VMEM)
@@ -300,19 +350,20 @@
                 pltpu.VMEM((CORES, 2, blk, head), F32),
                 pltpu.VMEM((seqs, 2, blk, head), BF16),
                 pltpu.VMEM((mine * 2 * cp, blk, head), BF16),
-                pltpu.VMEM((mine, head, CORES * rows), BF16),
-                pltpu.VMEM((head, CORES * rows), F32),
-                pltpu.VMEM((blk, rows), jnp.int32),
-                pltpu.VMEM((keys, CORES * rows), BF16),
-                pltpu.VMEM((keys, CORES * rows), F32),
+                pltpu.VMEM((mine, tiles, head, LANES), BF16),
+                pltpu.VMEM((tiles, head, LANES), F32),
+                pltpu.VMEM((tiles, blk, LANES), jnp.int32),
+                pltpu.VMEM((tiles, keys, LANES), BF16),
+                pltpu.VMEM((tiles, keys, LANES), F32),
                 pltpu.VMEM((1, CORES * rows), F32),
-                pltpu.VMEM((keys, CORES * rows), BF16),
-                pltpu.VMEM((mine, keys, CORES * rows), BF16),
-                pltpu.VMEM((mine, head, CORES * rows), BF16),
+                pltpu.VMEM((tiles, keys, LANES), BF16),
+                pltpu.VMEM((mine, tiles, keys, LANES), BF16),
+                pltpu.VMEM((mine, tiles, head, LANES), BF16),
                 pltpu.VMEM((mine * 2 * cp, blk, head), F32),
+                pltpu.VMEM((CORES * len(RELAYED), blk, head), F32),
                 pltpu.VMEM((mine, rows, head), BF16),
                 pltpu.VMEM((mine, rows, head), BF16),
-                dma((3,)), dma, dma, dma((mine,)), dma((2,)), dma, dma((mine, 2)), dma((2,)), dma((2,)),
+                dma((3,)), dma, dma, dma((mine,)), dma((2,)), dma, dma((mine, 2)), dma((2,)), dma, dma((2,)),
             ],
             compiler_params=pltpu.CompilerParams(collective_id=0, has_side_effects=True,
                                                  vmem_limit_bytes=32 * 2 ** 20),

time: 20 us -> 19.3 us (0.965)
  Pallas kernels: 19.2 us -> 18.5 us
    pallas_call x1, Pallas kernels: 17.9 us -> 17.2 us  [per_device(): pl.pallas_call(functools.partial(attend_kernel, cp, blk), out_shape=[big,...]
where the time goes in v3:
time: 19.3 us; the launch traced here: 19.2 us
  Pallas kernels  18.5 us (96%)
  between operations  0.64 us (3%)
    pallas_call x1, Pallas kernels, per_device(): pl.pallas_call(functools.partial(attend_kernel, cp, blk), out_shape=[big,...  17.2 us
    pallas_call x1, Pallas kernels, per_device(): pl.pallas_call(finish_kernel, out_shape=[big, big, small, small], in_spec...  1.36 us

profile of v3, /device:TPU:113, one launch (start us, length us, event | category | flops | bytes accessed | tf_op | source)
XLA Modules:
  0.0 19.2 jit_solution(13433803092099074906)
XLA Ops:
  0.6 17.2 %attend.1 = (bf16[4,1024,128]{2,1,0:T(8,128)(2,1)S(1)}, bf16[4,1024,128]{2,1,0:T(8,128)(2,1)S(1)}, f32[32,32,128]{2,1,0:T(8,128)S(1)}, f32[2,32,128]{2,1,0:T(8,128)S(1)}) custom-call(bf16[4,1024,128]{2,1,0:T(8,128)(2,1)} %bitcast.5, bf16[4,1024,128]{2,1,0:T(8,128)(2,1)} %bitcast.6, bf16[4,32,128]{2,1,0:T(8,128)(2,1)} %k_hbm.1, bf16[4,32,128]{2,1,0:T(8,128)(2,1)} %v_hbm.1, ...), custom_call_target="tpu_custom_call" | custom-call | tf_op jit(solution)/shard_map/attend/pallas_call | solution.py:338
  17.8 1.4 %finish.1 = (bf16[4,1024,128]{2,1,0:T(8,128)(2,1)}, bf16[4,1024,128]{2,1,0:T(8,128)(2,1)}, bf16[4,32,128]{2,1,0:T(8,128)(2,1)}, bf16[4,32,128]{2,1,0:T(8,128)(2,1)}) custom-call(bf16[4,1024,128]{2,1,0:T(8,128)(2,1)S(1)} %get-tuple-element.12.o_in, bf16[4,1024,128]{2,1,0:T(8,128)(2,1)S(1)} %get-tuple-element.13.dq_in, ...), custom_call_target="tpu_custom_call" | custom-call | tf_op jit(solution)/shard_map/finish/pallas_call | solution.py:374

commit v4 on v3

--- a/solution.py
+++ b/solution.py
@@ -15,7 +15,7 @@
 BF16 = jnp.bfloat16
 ROWS = 512
 LANES = 128
-RELAYED = (1,)
+RELAYED = (0,)
 
 
 def dot_nn(a, b):
@@ -28,18 +28,19 @@
 
 def put(ref, row0, val):
     for n in range(0, val.shape[1], LANES):
-        ref[(row0 + n) // LANES] = val[:, n:n + LANES]
-
-
-def get(ref, row0, count):
-    return jnp.concatenate([ref[(row0 + n) // LANES] for n in range(0, count, LANES)], axis=1)
+        ref[(row0 + n) // LANES, :val.shape[0]] = val[:, n:n + LANES]
+
+
+def get(ref, row0, count, height=None):
+    height = ref.shape[1] if height is None else height
+    return jnp.concatenate([ref[(row0 + n) // LANES, :height] for n in range(0, count, LANES)], axis=1)
 
 
 def attend_kernel(cp, blk, q_hbm, g_hbm, k_hbm, v_hbm, pos_hbm, freq_hbm,
                   o_ref, dq_ref, rbuf, tabs_out,
                   kv_in, pos_ref, freq_ref, qg, rq, tabs, kvown, kvb, g_t, tab_t, diff,
-                  w_t, p_f, norm, p_t, ds_t, o_t, part, passing, osib, dqsib,
-                  first_sem, loc_sem, qg_send, qg_recv, tab_sem, kv_send, kv_recv,
+                  x_s, w_t, p_f, norm, p_t, ds_t, o_t, part, passing, osib, dqsib,
+                  first_sem, loc_sem, qg_send, qg_recv, tab_sem, kv_send, kv_recv, far_recv,
                   r_sem, pass_sem, od_sem):
     chips = cp // CORES
     seqs = q_hbm.shape[0]
@@ -66,11 +67,15 @@
     def wait_bytes(ref, sem):
         pltpu.make_async_copy(ref, ref, sem).wait()
 
-    def wait_by_chip(ref, sem, blocks):
-        for c in range(chips):
-            @pl.when(chip == c)
-            def _():
-                wait_bytes(ref.at[pl.ds(0, blocks(c))], sem)
+    def wait_by_chip(ref, sem, blocks, last=None):
+        if last:
+            wait_bytes(ref.at[pl.ds(0, blocks(chips - 1))], sem)
+            return
+        for c in range(chips if last is None else chips - 1):
+            if blocks(c):
+                @pl.when(chip == c)
+                def _():
+                    wait_bytes(ref.at[pl.ds(0, blocks(c))], sem)
 
     first = [pltpu.make_async_copy(pos_hbm, pos_ref, first_sem.at[0]),
              pltpu.make_async_copy(freq_hbm, freq_ref, first_sem.at[1]),
@@ -98,6 +103,10 @@
         @pl.when(chip + d >= chips)
         def _():
             rbuf[d * seqs * 2:(d + 1) * seqs * 2] = jnp.zeros((seqs * 2, blk, head), F32)
+
+    @pl.when(chip < chips - 1)
+    def _():
+        ds_t[:, :, keys - CORES * blk:] = jnp.zeros((mine, ds_t.shape[1], CORES * blk, LANES), BF16)
 
     first[0].wait()
     first[1].wait()
@@ -126,12 +135,16 @@
             @pl.when(chip + d < chips)
             def _():
                 for k2 in range(CORES):
-                    remote(kvown.at[k2 * mine + s, n], kvb.at[base + d * CORES + core], kv_send, kv_recv.at[s, n],
+                    remote(kvown.at[k2 * mine + s, n], kvb.at[base + d * CORES + core], kv_send,
+                           far_recv if (s, n) == (0, 0) and d > 1 else kv_recv.at[s, n],
                            (chip + d) * CORES + k2).start()
         remote(kvown.at[(1 - core) * mine + s, n], kvb.at[base + core], kv_send, kv_recv.at[s, n], sib).start()
 
-    def kv_wait(s, n):
-        wait_by_chip(kvb, kv_recv.at[s, n], lambda c: CORES * c + 1)
+    def kv_wait(s, n, last):
+        wait_by_chip(kvb, kv_recv.at[s, n], lambda c: CORES * (min(c, 1) if (s, n) == (0, 0) else c) + 1, last)
+
+    def far_wait(last):
+        wait_by_chip(kvb, far_recv, lambda c: CORES * max(c - 1, 0), last)
 
     tab_copy = remote(tabs.at[0], tabs.at[1], tab_sem.at[0], tab_sem.at[1], sib)
 
@@ -185,14 +198,24 @@
             remote(part.at[base + d * CORES + k2], rbuf.at[d * seqs * 2 + slot], r_sem.at[0], r_sem.at[1],
                    (chip - d) * CORES + k2).start()
 
-    def send_part(s, x):
+    def send_near(s, x):
         base = (s * 2 + x) * cp
         slot = (core * mine + s) * 2 + x
+        remote(part.at[base + 1 - core], rbuf.at[slot], r_sem.at[0], r_sem.at[1], sib).start()
+        rbuf[slot] = part[base + core]
+
+    def send_part(s, x, last):
+        if last:
+            for d in (chips - 1, *range(1, chips - 1)):
+                send_far(s, x, d)
+            send_near(s, x)
+            return
+        base = (s * 2 + x) * cp
         relayed = s == 0 and x in RELAYED
-        for d in range(chips - 1, 0, -1):
+        for d in range(chips - 2, 0, -1):
             direct = chip >= d
             if relayed and d == origin:
-                direct = jnp.logical_and(direct, chip != origin)
+                direct = None
 
                 @pl.when(chip == origin)
                 def _():
@@ -202,31 +225,45 @@
                                middle * CORES + core).start()
             if relayed and d == middle:
                 direct = jnp.logical_and(direct, chip != middle)
-
-            @pl.when(direct)
-            def _():
-                send_far(s, x, d)
-        remote(part.at[base + 1 - core], rbuf.at[slot], r_sem.at[0], r_sem.at[1], sib).start()
-        rbuf[slot] = part[base + core]
+            if direct is not None:
+                @pl.when(direct)
+                def _():
+                    send_far(s, x, d)
+        send_near(s, x)
 
     def out_copy(src, dst, s):
         return remote(src.at[s], dst.at[core * mine + s], od_sem.at[0], od_sem.at[1], sib)
 
-    for s in range(mine):
-        kv_wait(s, 0)
-        kk = kvb[s * 2 * cp:(s * 2 + 1) * cp].reshape(keys, head)
-        for h in (0, 1):
-            owner = core if h == 0 else 1 - core
-            for r in range(0, rows, ROWS):
-                row0 = h * rows + r
-                x = dot_nt(kk, rq[s, row0:row0 + ROWS, :])
-                dif = get(diff, r, ROWS)
-                pieces = [jnp.where(dif <= (owner - k) * blk, x[k * blk:(k + 1) * blk], -jnp.inf)
-                          for k in range(CORES)]
-                for d in range(1, chips):
-                    bias = jnp.where(d <= chip, 0.0, -jnp.inf)
-                    pieces.append(x[d * CORES * blk:(d + 1) * CORES * blk] + bias)
-                x = jnp.concatenate(pieces, axis=0)
+    def scores(s, first_slot, slots, row0):
+        kk = kvb[s * 2 * cp + first_slot:s * 2 * cp + first_slot + slots].reshape(slots * blk, head)
+        x = dot_nt(kk, rq[s, row0:row0 + ROWS, :])
+        h, r = row0 // rows, row0 % rows
+        owner = core if h == 0 else 1 - core
+        dif = get(diff, r, ROWS)
+        pieces = []
+        for k in range(slots):
+            xk = x[k * blk:(k + 1) * blk]
+            if first_slot + k < CORES:
+                xk = jnp.where(dif <= (owner - k) * blk, xk, -jnp.inf)
+            else:
+                xk = xk + jnp.where((first_slot + k) // CORES <= chip, 0.0, -jnp.inf)
+            pieces.append(xk)
+        return jnp.concatenate(pieces, axis=0)
+
+    def pipeline(slots, last):
+        n_keys = slots * blk
+        near = 2 * CORES
+        for s in range(mine):
+            kv_wait(s, 0, last)
+            if s == 0:
+                for row0 in range(0, CORES * rows, ROWS):
+                    put(x_s, row0, scores(s, 0, near, row0))
+                far_wait(last)
+            for row0 in range(0, CORES * rows, ROWS):
+                if s == 0:
+                    x = jnp.concatenate([get(x_s, row0, ROWS), scores(s, near, slots - near, row0)], axis=0)
+                else:
+                    x = scores(s, 0, slots, row0)
                 mx = jnp.max(x, axis=0, keepdims=True)
                 w = jnp.exp2((x - mx) * (scale * LOG2E))
                 inv_l = 1.0 / jnp.sum(w, axis=0, keepdims=True)
@@ -235,22 +272,29 @@
                 put(p_f, row0, p)
                 put(p_t, row0, p.astype(BF16))
                 norm[:, row0:row0 + ROWS] = inv_l
-        part[(s * 2 + 1) * cp:(s * 2 + 2) * cp] = dot_nn(
-            get(p_t, 0, CORES * rows), qg[1, s].reshape(CORES * rows, head)).reshape(cp, blk, head)
-        send_part(s, 1)
-        kv_wait(s, 1)
-        vv = kvb[(s * 2 + 1) * cp:(s * 2 + 2) * cp].reshape(keys, head)
-        v_t = vv.T
-        for h in (0, 1):
-            for r in range(0, rows, ROWS):
-                row0 = h * rows + r
-                ot = (dot_nn(v_t, get(w_t, row0, ROWS)) * norm[:, row0:row0 + ROWS]).astype(BF16)
+            at = (s * 2 + 1) * cp
+            part[at:at + slots] = dot_nn(get(p_t, 0, CORES * rows, n_keys),
+                                         qg[1, s].reshape(CORES * rows, head)).reshape(slots, blk, head)
+            send_part(s, 1, last)
+            kv_wait(s, 1, last)
+            vv = kvb[at:at + slots].reshape(n_keys, head)
+            v_t = vv.T
+            for row0 in range(0, CORES * rows, ROWS):
+                ot = (dot_nn(v_t, get(w_t, row0, ROWS, n_keys)) * norm[:, row0:row0 + ROWS]).astype(BF16)
                 put(o_t.at[s], row0, ot)
                 delta = jnp.sum(get(g_t.at[s], row0, ROWS).astype(F32) * ot.astype(F32), axis=0, keepdims=True)
-                dp = dot_nt(vv, qg[1, s, h, r:r + ROWS, :])
-                put(ds_t.at[s], row0, (get(p_f, row0, ROWS) * (dp - delta)).astype(BF16))
-        part[s * 2 * cp:(s * 2 + 1) * cp] = dot_nn(get(ds_t.at[s], 0, CORES * rows), rq[s]).reshape(cp, blk, head)
-        send_part(s, 0)
+                dp = dot_nt(vv, qg[1, s, row0 // rows, row0 % rows:row0 % rows + ROWS, :])
+                put(ds_t.at[s], row0, (get(p_f, row0, ROWS, n_keys) * (dp - delta)).astype(BF16))
+            at = s * 2 * cp
+            part[at:at + slots] = dot_nn(get(ds_t.at[s], 0, CORES * rows, n_keys), rq[s]).reshape(slots, blk, head)
+            send_part(s, 0, last)
+    @pl.when(chip == chips - 1)
+    def _():
+        pipeline(cp, True)
+
+    @pl.when(chip < chips - 1)
+    def _():
+        pipeline(cp - CORES, False)
 
     @pl.when(chip == middle)
     def _():
@@ -353,6 +397,7 @@
                 pltpu.VMEM((mine, tiles, head, LANES), BF16),
                 pltpu.VMEM((tiles, head, LANES), F32),
                 pltpu.VMEM((tiles, blk, LANES), jnp.int32),
+                pltpu.VMEM((tiles, 2 * CORES * blk, LANES), F32),
                 pltpu.VMEM((tiles, keys, LANES), BF16),
                 pltpu.VMEM((tiles, keys, LANES), F32),
                 pltpu.VMEM((1, CORES * rows), F32),
@@ -363,7 +408,7 @@
                 pltpu.VMEM((CORES * len(RELAYED), blk, head), F32),
                 pltpu.VMEM((mine, rows, head), BF16),
                 pltpu.VMEM((mine, rows, head), BF16),
-                dma((3,)), dma, dma, dma((mine,)), dma((2,)), dma, dma((mine, 2)), dma((2,)), dma, dma((2,)),
+                dma((3,)), dma, dma, dma((mine,)), dma((2,)), dma, dma((mine, 2)), dma, dma((2,)), dma, dma((2,)),
             ],
             compiler_params=pltpu.CompilerParams(collective_id=0, has_side_effects=True,
                                                  vmem_limit_bytes=32 * 2 ** 20),

time: 19.3 us -> 18.5 us (0.959)
  Pallas kernels: 18.5 us -> 17.8 us
    pallas_call x1, Pallas kernels: 17.2 us -> 16.4 us  [per_device(): pl.pallas_call(functools.partial(attend_kernel, cp, blk), out_shape=[big,...]
where the time goes in v4:
time: 18.5 us; the launch traced here: 18.4 us
  Pallas kernels  17.8 us (96%)
  between operations  0.64 us (3%)
    pallas_call x1, Pallas kernels, per_device(): pl.pallas_call(functools.partial(attend_kernel, cp, blk), out_shape=[big,...  16.4 us
    pallas_call x1, Pallas kernels, per_device(): pl.pallas_call(finish_kernel, out_shape=[big, big, small, small], in_spec...  1.36 us

profile of v4, /device:TPU:113, one launch (start us, length us, event | category | flops | bytes accessed | tf_op | source)
XLA Modules:
  0.0 18.4 jit_solution(9727461568043992152)
XLA Ops:
  0.6 16.4 %attend.1 = (bf16[4,1024,128]{2,1,0:T(8,128)(2,1)S(1)}, bf16[4,1024,128]{2,1,0:T(8,128)(2,1)S(1)}, f32[32,32,128]{2,1,0:T(8,128)S(1)}, f32[2,32,128]{2,1,0:T(8,128)S(1)}) custom-call(bf16[4,1024,128]{2,1,0:T(8,128)(2,1)} %bitcast.5, bf16[4,1024,128]{2,1,0:T(8,128)(2,1)} %bitcast.6, bf16[4,32,128]{2,1,0:T(8,128)(2,1)} %k_hbm.1, bf16[4,32,128]{2,1,0:T(8,128)(2,1)} %v_hbm.1, ...), custom_call_target="tpu_custom_call" | custom-call | tf_op jit(solution)/shard_map/attend/pallas_call | solution.py:382
  17.1 1.4 %finish.1 = (bf16[4,1024,128]{2,1,0:T(8,128)(2,1)}, bf16[4,1024,128]{2,1,0:T(8,128)(2,1)}, bf16[4,32,128]{2,1,0:T(8,128)(2,1)}, bf16[4,32,128]{2,1,0:T(8,128)(2,1)}) custom-call(bf16[4,1024,128]{2,1,0:T(8,128)(2,1)S(1)} %get-tuple-element.12.o_in, bf16[4,1024,128]{2,1,0:T(8,128)(2,1)S(1)} %get-tuple-element.13.dq_in, ...), custom_call_target="tpu_custom_call" | custom-call | tf_op jit(solution)/shard_map/finish/pallas_call | solution.py:419

commit v5 on v4

--- a/solution.py
+++ b/solution.py
@@ -39,7 +39,7 @@
 def attend_kernel(cp, blk, q_hbm, g_hbm, k_hbm, v_hbm, pos_hbm, freq_hbm,
                   o_ref, dq_ref, rbuf, tabs_out,
                   kv_in, pos_ref, freq_ref, qg, rq, tabs, kvown, kvb, g_t, tab_t, diff,
-                  x_s, w_t, p_f, norm, p_t, ds_t, o_t, part, passing, osib, dqsib,
+                  w_s, run_max, w_t, p_f, norm, p_t, ds_t, o_t, part, passing, osib, dqsib,
                   first_sem, loc_sem, qg_send, qg_recv, tab_sem, kv_send, kv_recv, far_recv,
                   r_sem, pass_sem, od_sem):
     chips = cp // CORES
@@ -257,16 +257,27 @@
             kv_wait(s, 0, last)
             if s == 0:
                 for row0 in range(0, CORES * rows, ROWS):
-                    put(x_s, row0, scores(s, 0, near, row0))
+                    x = scores(s, 0, near, row0)
+                    mx = jnp.max(x, axis=0, keepdims=True)
+                    w = jnp.exp2((x - mx) * (scale * LOG2E))
+                    put(w_s, row0, w)
+                    run_max[:, row0:row0 + ROWS] = mx
+                    norm[:, row0:row0 + ROWS] = jnp.sum(w, axis=0, keepdims=True)
                 far_wait(last)
             for row0 in range(0, CORES * rows, ROWS):
                 if s == 0:
-                    x = jnp.concatenate([get(x_s, row0, ROWS), scores(s, near, slots - near, row0)], axis=0)
+                    x = scores(s, near, slots - near, row0)
+                    mx_near = run_max[:, row0:row0 + ROWS]
+                    mx = jnp.maximum(mx_near, jnp.max(x, axis=0, keepdims=True))
+                    factor = jnp.exp2((mx_near - mx) * (scale * LOG2E))
+                    w = jnp.exp2((x - mx) * (scale * LOG2E))
+                    inv_l = 1.0 / (norm[:, row0:row0 + ROWS] * factor + jnp.sum(w, axis=0, keepdims=True))
+                    w = jnp.concatenate([get(w_s, row0, ROWS) * factor, w], axis=0)
                 else:
                     x = scores(s, 0, slots, row0)
-                mx = jnp.max(x, axis=0, keepdims=True)
-                w = jnp.exp2((x - mx) * (scale * LOG2E))
-                inv_l = 1.0 / jnp.sum(w, axis=0, keepdims=True)
+                    mx = jnp.max(x, axis=0, keepdims=True)
+                    w = jnp.exp2((x - mx) * (scale * LOG2E))
+                    inv_l = 1.0 / jnp.sum(w, axis=0, keepdims=True)
                 put(w_t, row0, w.astype(BF16))
                 p = w * inv_l
                 put(p_f, row0, p)
@@ -398,6 +409,7 @@
                 pltpu.VMEM((tiles, head, LANES), F32),
                 pltpu.VMEM((tiles, blk, LANES), jnp.int32),
                 pltpu.VMEM((tiles, 2 * CORES * blk, LANES), F32),
+                pltpu.VMEM((1, CORES * rows), F32),
                 pltpu.VMEM((tiles, keys, LANES), BF16),
                 pltpu.VMEM((tiles, keys, LANES), F32),
                 pltpu.VMEM((1, CORES * rows), F32),

time: 18.5 us -> 18.4 us (level)
  no operation moved by 1% of the time
where the time goes in v5:
time: 18.4 us; the launch traced here: 18.3 us
  Pallas kernels  17.7 us (96%)
  between operations  0.64 us (3%)
    pallas_call x1, Pallas kernels, per_device(): pl.pallas_call(functools.partial(attend_kernel, cp, blk), out_shape=[big,...  16.3 us
    pallas_call x1, Pallas kernels, per_device(): pl.pallas_call(finish_kernel, out_shape=[big, big, small, small], in_spec...  1.36 us

profile of v5, /device:TPU:113, one launch (start us, length us, event | category | flops | bytes accessed | tf_op | source)
XLA Modules:
  0.0 18.3 jit_solution(17071565890757206303)
XLA Ops:
  0.6 16.3 %attend.1 = (bf16[4,1024,128]{2,1,0:T(8,128)(2,1)S(1)}, bf16[4,1024,128]{2,1,0:T(8,128)(2,1)S(1)}, f32[32,32,128]{2,1,0:T(8,128)S(1)}, f32[2,32,128]{2,1,0:T(8,128)S(1)}) custom-call(bf16[4,1024,128]{2,1,0:T(8,128)(2,1)} %bitcast.5, bf16[4,1024,128]{2,1,0:T(8,128)(2,1)} %bitcast.6, bf16[4,32,128]{2,1,0:T(8,128)(2,1)} %k_hbm.1, bf16[4,32,128]{2,1,0:T(8,128)(2,1)} %v_hbm.1, ...), custom_call_target="tpu_custom_call" | custom-call | tf_op jit(solution)/shard_map/attend/pallas_call | solution.py:393
  16.9 1.4 %finish.1 = (bf16[4,1024,128]{2,1,0:T(8,128)(2,1)}, bf16[4,1024,128]{2,1,0:T(8,128)(2,1)}, bf16[4,32,128]{2,1,0:T(8,128)(2,1)}, bf16[4,32,128]{2,1,0:T(8,128)(2,1)}) custom-call(bf16[4,1024,128]{2,1,0:T(8,128)(2,1)S(1)} %get-tuple-element.12.o_in, bf16[4,1024,128]{2,1,0:T(8,128)(2,1)S(1)} %get-tuple-element.13.dq_in, ...), custom_call_target="tpu_custom_call" | custom-call | tf_op jit(solution)/shard_map/finish/pallas_call | solution.py:431

commit v6 on v5

--- a/solution.py
+++ b/solution.py
@@ -181,12 +181,12 @@
     tab_copy.wait_recv()
     cs = tables(1)
     for s in range(mine):
+        if s + 1 < mine:
+            kv_wave(s + 1, 0)
         wait_bytes(qg.at[0, 0], qg_recv.at[s])
         prepare(s, 1, *cs)
         if s + 1 < mine:
-            kv_wave(s + 1, 0)
-    for s in range(1, mine):
-        kv_wave(s, 1)
+            kv_wave(s + 1, 1)
 
     origin = chips - 2
     middle = origin - 1
@@ -234,7 +234,7 @@
     def out_copy(src, dst, s):
         return remote(src.at[s], dst.at[core * mine + s], od_sem.at[0], od_sem.at[1], sib)
 
-    def scores(s, first_slot, slots, row0):
+    def scores(s, first_slot, slots, row0, last):
         kk = kvb[s * 2 * cp + first_slot:s * 2 * cp + first_slot + slots].reshape(slots * blk, head)
         x = dot_nt(kk, rq[s, row0:row0 + ROWS, :])
         h, r = row0 // rows, row0 % rows
@@ -245,7 +245,7 @@
             xk = x[k * blk:(k + 1) * blk]
             if first_slot + k < CORES:
                 xk = jnp.where(dif <= (owner - k) * blk, xk, -jnp.inf)
-            else:
+            elif not last:
                 xk = xk + jnp.where((first_slot + k) // CORES <= chip, 0.0, -jnp.inf)
             pieces.append(xk)
         return jnp.concatenate(pieces, axis=0)
@@ -257,7 +257,7 @@
             kv_wait(s, 0, last)
             if s == 0:
                 for row0 in range(0, CORES * rows, ROWS):
-                    x = scores(s, 0, near, row0)
+                    x = scores(s, 0, near, row0, last)
                     mx = jnp.max(x, axis=0, keepdims=True)
                     w = jnp.exp2((x - mx) * (scale * LOG2E))
                     put(w_s, row0, w)
@@ -266,7 +266,7 @@
                 far_wait(last)
             for row0 in range(0, CORES * rows, ROWS):
                 if s == 0:
-                    x = scores(s, near, slots - near, row0)
+                    x = scores(s, near, slots - near, row0, last)
                     mx_near = run_max[:, row0:row0 + ROWS]
                     mx = jnp.maximum(mx_near, jnp.max(x, axis=0, keepdims=True))
                     factor = jnp.exp2((mx_near - mx) * (scale * LOG2E))
@@ -274,7 +274,7 @@
                     inv_l = 1.0 / (norm[:, row0:row0 + ROWS] * factor + jnp.sum(w, axis=0, keepdims=True))
                     w = jnp.concatenate([get(w_s, row0, ROWS) * factor, w], axis=0)
                 else:
-                    x = scores(s, 0, slots, row0)
+                    x = scores(s, 0, slots, row0, last)
                     mx = jnp.max(x, axis=0, keepdims=True)
                     w = jnp.exp2((x - mx) * (scale * LOG2E))
                     inv_l = 1.0 / jnp.sum(w, axis=0, keepdims=True)

time: 18.4 us -> 18.3 us (level)
  no operation moved by 1% of the time
where the time goes in v6:
time: 18.3 us; the launch traced here: 18.2 us
  Pallas kernels  17.6 us (96%)
  between operations  0.64 us (3%)
    pallas_call x1, Pallas kernels, per_device(): pl.pallas_call(functools.partial(attend_kernel, cp, blk), out_shape=[big,...  16.2 us
    pallas_call x1, Pallas kernels, per_device(): pl.pallas_call(finish_kernel, out_shape=[big, big, small, small], in_spec...  1.36 us

profile of v6, /device:TPU:113, one launch (start us, length us, event | category | flops | bytes accessed | tf_op | source)
XLA Modules:
  0.0 18.2 jit_solution(3861986313107399539)
XLA Ops:
  0.6 16.2 %attend.1 = (bf16[4,1024,128]{2,1,0:T(8,128)(2,1)S(1)}, bf16[4,1024,128]{2,1,0:T(8,128)(2,1)S(1)}, f32[32,32,128]{2,1,0:T(8,128)S(1)}, f32[2,32,128]{2,1,0:T(8,128)S(1)}) custom-call(bf16[4,1024,128]{2,1,0:T(8,128)(2,1)} %bitcast.5, bf16[4,1024,128]{2,1,0:T(8,128)(2,1)} %bitcast.6, bf16[4,32,128]{2,1,0:T(8,128)(2,1)} %k_hbm.1, bf16[4,32,128]{2,1,0:T(8,128)(2,1)} %v_hbm.1, ...), custom_call_target="tpu_custom_call" | custom-call | tf_op jit(solution)/shard_map/attend/pallas_call | solution.py:393
  16.9 1.4 %finish.1 = (bf16[4,1024,128]{2,1,0:T(8,128)(2,1)}, bf16[4,1024,128]{2,1,0:T(8,128)(2,1)}, bf16[4,32,128]{2,1,0:T(8,128)(2,1)}, bf16[4,32,128]{2,1,0:T(8,128)(2,1)}) custom-call(bf16[4,1024,128]{2,1,0:T(8,128)(2,1)S(1)} %get-tuple-element.12.o_in, bf16[4,1024,128]{2,1,0:T(8,128)(2,1)S(1)} %get-tuple-element.13.dq_in, ...), custom_call_target="tpu_custom_call" | custom-call | tf_op jit(solution)/shard_map/finish/pallas_call | solution.py:431

commit v7 on v6

--- a/solution.py
+++ b/solution.py
@@ -194,7 +194,7 @@
     def send_far(s, x, d):
         base = (s * 2 + x) * cp
         slot = (core * mine + s) * 2 + x
-        for k2 in range(CORES):
+        for k2 in reversed(range(CORES)):
             remote(part.at[base + d * CORES + k2], rbuf.at[d * seqs * 2 + slot], r_sem.at[0], r_sem.at[1],
                    (chip - d) * CORES + k2).start()
 
@@ -225,11 +225,18 @@
                                middle * CORES + core).start()
             if relayed and d == middle:
                 direct = jnp.logical_and(direct, chip != middle)
+            if s == 0 and d == 1:
+                direct = jnp.logical_and(direct, chip != origin)
             if direct is not None:
                 @pl.when(direct)
                 def _():
                     send_far(s, x, d)
         send_near(s, x)
+        if (s, x) == (1, 1):
+            @pl.when(chip == origin)
+            def _():
+                for late in (1, 0):
+                    send_far(0, late, 1)
 
     def out_copy(src, dst, s):
         return remote(src.at[s], dst.at[core * mine + s], od_sem.at[0], od_sem.at[1], sib)

time: 18.3 us -> 18.3 us (level)
  no operation moved by 1% of the time
where the time goes in v7:
time: 18.3 us; the launch traced here: 18.1 us
  Pallas kernels  17.5 us (96%)
  between operations  0.64 us (3%)
    pallas_call x1, Pallas kernels, per_device(): pl.pallas_call(functools.partial(attend_kernel, cp, blk), out_shape=[big,...  16.1 us
    pallas_call x1, Pallas kernels, per_device(): pl.pallas_call(finish_kernel, out_shape=[big, big, small, small], in_spec...  1.36 us

profile of v7, /device:TPU:113, one launch (start us, length us, event | category | flops | bytes accessed | tf_op | source)
XLA Modules:
  0.0 18.1 jit_solution(16069791325093270969)
XLA Ops:
  0.6 16.1 %attend.1 = (bf16[4,1024,128]{2,1,0:T(8,128)(2,1)S(1)}, bf16[4,1024,128]{2,1,0:T(8,128)(2,1)S(1)}, f32[32,32,128]{2,1,0:T(8,128)S(1)}, f32[2,32,128]{2,1,0:T(8,128)S(1)}) custom-call(bf16[4,1024,128]{2,1,0:T(8,128)(2,1)} %bitcast.5, bf16[4,1024,128]{2,1,0:T(8,128)(2,1)} %bitcast.6, bf16[4,32,128]{2,1,0:T(8,128)(2,1)} %k_hbm.1, bf16[4,32,128]{2,1,0:T(8,128)(2,1)} %v_hbm.1, ...), custom_call_target="tpu_custom_call" | custom-call | tf_op jit(solution)/shard_map/attend/pallas_call | solution.py:400
  16.8 1.4 %finish.1 = (bf16[4,1024,128]{2,1,0:T(8,128)(2,1)}, bf16[4,1024,128]{2,1,0:T(8,128)(2,1)}, bf16[4,32,128]{2,1,0:T(8,128)(2,1)}, bf16[4,32,128]{2,1,0:T(8,128)(2,1)}) custom-call(bf16[4,1024,128]{2,1,0:T(8,128)(2,1)S(1)} %get-tuple-element.12.o_in, bf16[4,1024,128]{2,1,0:T(8,128)(2,1)S(1)} %get-tuple-element.13.dq_in, ...), custom_call_target="tpu_custom_call" | custom-call | tf_op jit(solution)/shard_map/finish/pallas_call | solution.py:438

commit v8 on v7

--- a/solution.py
+++ b/solution.py
@@ -40,7 +40,7 @@
                   o_ref, dq_ref, rbuf, tabs_out,
                   kv_in, pos_ref, freq_ref, qg, rq, tabs, kvown, kvb, g_t, tab_t, diff,
                   w_s, run_max, w_t, p_f, norm, p_t, ds_t, o_t, part, passing, osib, dqsib,
-                  first_sem, loc_sem, qg_send, qg_recv, tab_sem, kv_send, kv_recv, far_recv,
+                  first_sem, loc_sem, qg_recv, tab_sem, kv_recv, far_recv,
                   r_sem, pass_sem, od_sem):
     chips = cp // CORES
     seqs = q_hbm.shape[0]
@@ -135,10 +135,10 @@
             @pl.when(chip + d < chips)
             def _():
                 for k2 in range(CORES):
-                    remote(kvown.at[k2 * mine + s, n], kvb.at[base + d * CORES + core], kv_send,
+                    remote(kvown.at[k2 * mine + s, n], kvb.at[base + d * CORES + core], r_sem.at[0],
                            far_recv if (s, n) == (0, 0) and d > 1 else kv_recv.at[s, n],
                            (chip + d) * CORES + k2).start()
-        remote(kvown.at[(1 - core) * mine + s, n], kvb.at[base + core], kv_send, kv_recv.at[s, n], sib).start()
+        remote(kvown.at[(1 - core) * mine + s, n], kvb.at[base + core], r_sem.at[0], kv_recv.at[s, n], sib).start()
 
     def kv_wait(s, n, last):
         wait_by_chip(kvb, kv_recv.at[s, n], lambda c: CORES * (min(c, 1) if (s, n) == (0, 0) else c) + 1, last)
@@ -146,13 +146,13 @@
     def far_wait(last):
         wait_by_chip(kvb, far_recv, lambda c: CORES * max(c - 1, 0), last)
 
-    tab_copy = remote(tabs.at[0], tabs.at[1], tab_sem.at[0], tab_sem.at[1], sib)
+    tab_copy = remote(tabs.at[0], tabs.at[1], r_sem.at[0], tab_sem, sib)
 
     kv_wave(0, 0)
     tab_copy.start()
     for s in range(mine):
         for n, src in enumerate((q_hbm, g_hbm)):
-            remote(src.at[(1 - core) * mine + s], qg.at[n, s, 1], qg_send, qg_recv.at[s], sib).start()
+            remote(src.at[(1 - core) * mine + s], qg.at[n, s, 1], od_sem.at[0], qg_recv.at[s], sib).start()
     for s in range(mine):
         for n in range(2):
             kvb[(s * 2 + n) * cp + core] = kvown[core * mine + s, n]
@@ -343,12 +343,9 @@
                 out_copy(osib, o_ref, s).start()
                 out_copy(dqsib, dq_ref, s).start()
 
-    tab_copy.wait_send()
-    wait_bytes(qg.at[0], qg_send)
-    wait_by_chip(kvb, kv_send, lambda c: 2 * mine * (CORES * (chips - 1 - c) + 1))
-    wait_bytes(qg.at[0], od_sem.at[0])
+    wait_bytes(qg, od_sem.at[0])
     wait_bytes(qg.at[0], od_sem.at[1])
-    wait_by_chip(part, r_sem.at[0], lambda c: 2 * mine * (CORES * c + 1))
+    wait_by_chip(part, r_sem.at[0], lambda c: 2 * mine * (CORES * c + 1) + mine * (CORES * (chips - 1 - c) + 1) + 2)
     wait_by_chip(rbuf, r_sem.at[1], lambda c: 2 * mine * (CORES * (chips - 1 - c) + 1)
                  - (CORES * len(RELAYED) if c == 0 else 0))
 
@@ -427,7 +424,7 @@
                 pltpu.VMEM((CORES * len(RELAYED), blk, head), F32),
                 pltpu.VMEM((mine, rows, head), BF16),
                 pltpu.VMEM((mine, rows, head), BF16),
-                dma((3,)), dma, dma, dma((mine,)), dma((2,)), dma, dma((mine, 2)), dma, dma((2,)), dma, dma((2,)),
+                dma((3,)), dma, dma((mine,)), dma, dma((mine, 2)), dma, dma((2,)), dma, dma((2,)),
             ],
             compiler_params=pltpu.CompilerParams(collective_id=0, has_side_effects=True,
                                                  vmem_limit_bytes=32 * 2 ** 20),

time: 18.3 us -> 18.2 us (level)
  no operation moved by 1% of the time
where the time goes in v8:
time: 18.2 us; the launch traced here: 18.1 us
  Pallas kernels  17.5 us (96%)
  between operations  0.64 us (4%)
    pallas_call x1, Pallas kernels, per_device(): pl.pallas_call(functools.partial(attend_kernel, cp, blk), out_shape=[big,...  16.1 us
    pallas_call x1, Pallas kernels, per_device(): pl.pallas_call(finish_kernel, out_shape=[big, big, small, small], in_spec...  1.36 us

profile of v8, /device:TPU:113, one launch (start us, length us, event | category | flops | bytes accessed | tf_op | source)
XLA Modules:
  0.0 18.1 jit_solution(6244733744320919919)
XLA Ops:
  0.6 16.1 %attend.1 = (bf16[4,1024,128]{2,1,0:T(8,128)(2,1)S(1)}, bf16[4,1024,128]{2,1,0:T(8,128)(2,1)S(1)}, f32[32,32,128]{2,1,0:T(8,128)S(1)}, f32[2,32,128]{2,1,0:T(8,128)S(1)}) custom-call(bf16[4,1024,128]{2,1,0:T(8,128)(2,1)} %bitcast.5, bf16[4,1024,128]{2,1,0:T(8,128)(2,1)} %bitcast.6, bf16[4,32,128]{2,1,0:T(8,128)(2,1)} %k_hbm.1, bf16[4,32,128]{2,1,0:T(8,128)(2,1)} %v_hbm.1, ...), custom_call_target="tpu_custom_call" | custom-call | tf_op jit(solution)/shard_map/attend/pallas_call | solution.py:397
  16.8 1.4 %finish.1 = (bf16[4,1024,128]{2,1,0:T(8,128)(2,1)}, bf16[4,1024,128]{2,1,0:T(8,128)(2,1)}, bf16[4,32,128]{2,1,0:T(8,128)(2,1)}, bf16[4,32,128]{2,1,0:T(8,128)(2,1)}) custom-call(bf16[4,1024,128]{2,1,0:T(8,128)(2,1)S(1)} %get-tuple-element.12.o_in, bf16[4,1024,128]{2,1,0:T(8,128)(2,1)S(1)} %get-tuple-element.13.dq_in, ...), custom_call_target="tpu_custom_call" | custom-call | tf_op jit(solution)/shard_map/finish/pallas_call | solution.py:435
